TPU v7x, 8 devices: a whole 2x2x1 slice. The times are simulated.
8 devices in a mesh: m: 1 (over z), kk: 2 (over y), g: 4 (over x, core).
Axes of the slice: x: 2, y: 2, z: 1, core: 2. Of those that a mesh axis runs over, the one named last changes fastest.
Arguments:
- a_mat: bfloat16 [8, 4096, 14336], P(None, ('m', 'g'), 'kk')
Outputs:
- output: float32 [4, 3, 8, 1024, 1024], P(('m', 'g'))
All inputs are finite; a program needn't handle non-finite values.
Results may differ from a plain program's by a relative error of at most 0.001.
Values are sent between devices in bfloat16 or wider.
A program may use at most 1 GiB of HBM per device.

v0:
```python
import jax
import jax.numpy as jnp
from jax import lax
from jax.sharding import PartitionSpec as P


def assignment_table(groups):
    slot_count = groups // 2 + 1
    log_two = groups.bit_length() - 1
    side_len = 2 ** (log_two // 2)
    dup_count = groups // (side_len * side_len)
    grp_width = groups // side_len
    piece_len = max(1, grp_width // (2 * dup_count))
    pair_lists = [[] for device_no in range(groups)]
    block_sets = [set() for device_no in range(groups)]
    spill_pairs = []
    for upper_grp in range(side_len):
        for lower_grp in range(upper_grp):
            for left_row in range(upper_grp * grp_width, (upper_grp + 1) * grp_width):
                part_no = (left_row % grp_width) // piece_len
                if part_no < dup_count:
                    target = dup_count * (upper_grp * side_len + lower_grp) + part_no
                else:
                    target = dup_count * (lower_grp * side_len + upper_grp) + part_no - dup_count
                for right_row in range(lower_grp * grp_width, (lower_grp + 1) * grp_width):
                    pair_lists[target].append((left_row, right_row))
                    block_sets[target].update([left_row, right_row])
    for diag_grp in range(side_len):
        first_dev = dup_count * (diag_grp * side_len + diag_grp)
        for left_row in range(diag_grp * grp_width, (diag_grp + 1) * grp_width):
            for right_row in range(diag_grp * grp_width, left_row + 1):
                target = -1
                for copy_no in range(dup_count):
                    if target < 0 and len(pair_lists[first_dev + copy_no]) < slot_count:
                        target = first_dev + copy_no
                if target < 0:
                    spill_pairs.append((left_row, right_row))
                else:
                    pair_lists[target].append((left_row, right_row))
                    block_sets[target].update([left_row, right_row])
    for (left_row, right_row) in spill_pairs:
        best_score = (3, groups + 1, groups)
        for device_no in range(groups):
            if len(pair_lists[device_no]) < slot_count:
                growth = len(set([left_row, right_row]) - block_sets[device_no])
                cand_score = (growth, len(pair_lists[device_no]), device_no)
                best_score = min(best_score, cand_score)
        target = best_score[2]
        pair_lists[target].append((left_row, right_row))
        block_sets[target].update([left_row, right_row])
    return pair_lists, block_sets


def fetch_plan(groups):
    pair_lists, block_sets = assignment_table(groups)
    slot_count = groups // 2 + 1
    src_color = {}
    dst_color = {}
    for receiver in range(groups):
        for sender in sorted(block_sets[receiver]):
            if sender != receiver:
                color_a = 0
                while (sender, color_a) in src_color:
                    color_a += 1
                color_b = 0
                while (receiver, color_b) in dst_color:
                    color_b += 1
                if (receiver, color_a) in dst_color:
                    path_edges = []
                    node_no = receiver
                    wanted = color_a
                    at_receiver = True
                    found_node = dst_color.get((node_no, wanted))
                    while found_node is not None:
                        if at_receiver:
                            path_edges.append((found_node, node_no, wanted))
                        else:
                            path_edges.append((node_no, found_node, wanted))
                        node_no = found_node
                        at_receiver = not at_receiver
                        wanted = color_b if wanted == color_a else color_a
                        if at_receiver:
                            found_node = dst_color.get((node_no, wanted))
                        else:
                            found_node = src_color.get((node_no, wanted))
                    for (from_dev, to_dev, color_no) in path_edges:
                        src_color.pop((from_dev, color_no))
                        dst_color.pop((to_dev, color_no))
                    for (from_dev, to_dev, color_no) in path_edges:
                        new_color = color_b if color_no == color_a else color_a
                        src_color[(from_dev, new_color)] = to_dev
                        dst_color[(to_dev, new_color)] = from_dev
                src_color[(sender, color_a)] = receiver
                dst_color[(receiver, color_a)] = sender
    round_count = 1 + max([color_no for (node_no, color_no) in src_color])
    rounds = [sorted([(from_dev, to_dev) for ((from_dev, color_no), to_dev) in src_color.items() if color_no == round_no]) for round_no in range(round_count)]
    left_slot = []
    right_slot = []
    live_flags = []
    for device_no in range(groups):
        slot_map = {device_no: 0}
        for round_no in range(round_count):
            if (device_no, round_no) in dst_color:
                slot_map[dst_color[(device_no, round_no)]] = 1 + round_no
        own_pairs = pair_lists[device_no]
        left_slot.append([slot_map[own_pairs[slot_no][0]] if slot_no < len(own_pairs) else 0 for slot_no in range(slot_count)])
        right_slot.append([slot_map[own_pairs[slot_no][1]] if slot_no < len(own_pairs) else 0 for slot_no in range(slot_count)])
        live_flags.append([1 if slot_no < len(own_pairs) else 0 for slot_no in range(slot_count)])
    return rounds, left_slot, right_slot, live_flags


def solution(mesh):
    groups = mesh.shape["g"]
    rounds, left_slot, right_slot, live_flags = fetch_plan(groups)

    def local_part(a_loc):
        layer_count, block_rows, k_cols = a_loc.shape
        dev_index = lax.axis_index("g")
        received = [lax.ppermute(a_loc, "g", round_pairs) for round_pairs in rounds]
        held_blocks = jnp.stack([a_loc] + received, axis=0)
        left_slots = jnp.array(left_slot, jnp.int32)[dev_index]
        right_slots = jnp.array(right_slot, jnp.int32)[dev_index]
        live_slots = jnp.array(live_flags, jnp.int32)[dev_index]

        def one_slot(slot_args):
            left_no, right_no, live_flag = slot_args

            def compute():
                left_blk = lax.dynamic_index_in_dim(held_blocks, left_no, 0, keepdims=False)
                right_blk = lax.dynamic_index_in_dim(held_blocks, right_no, 0, keepdims=False)
                return jnp.einsum("lbk,lck->lbc", left_blk, right_blk, preferred_element_type=jnp.float32)

            def skip_slot():
                return jnp.zeros((layer_count, block_rows, block_rows), jnp.float32)

            return lax.cond(live_flag == 1, compute, skip_slot)

        partial_sums = lax.map(one_slot, (left_slots, right_slots, live_slots))
        totals = lax.psum(partial_sums, "kk")
        return totals[None]

    return jax.shard_map(local_part, mesh=mesh, in_specs=(P(None, ("m", "g"), "kk"),), out_specs=P(("m", "g"), None, None, None, None), check_vma=False)
```

profile of v0, /device:TPU:1, one launch (start us, length us, event | category | flops | bytes accessed | tf_op | source)
XLA Modules:
  0.0 5490.6 jit_solution(293493956812919220)
XLA Ops:
  6.5 0.0 all-reduce.2.cloned.1.call-start
  6.5 4.5 collective-permute-start.1
  11.0 33.7 collective-permute-start
  44.7 1.2 fusion.13
  45.9 1.2 fusion.11
  47.2 2447.2 %collective-permute-done.1 = bf16[8,1024,7168]{2,1,0:T(8,128)(2,1)} collective-permute-done((bf16[8,1024,7168]{2,1,0:T(8,128)(2,1)}, bf16[8,1024,7168]{2,1,0:T(8,128)(2,1)}, u32[]{:S(2)}, u32[]{:S(2)}) %collective-permute-start.1) | collective-permute-done | bytes 117440544 | tf_op jit(solution)/shard_map/ppermute | solution.py:119
  2494.3 0.0 collective-permute-done
  2494.3 0.0 copy-start
  2494.3 0.0 copy-start.2
  2494.4 0.0 copy-start.3
  2494.4 229.6 %pad_maximum_fusion = bf16[3,8,1024,7168]{3,2,1,0:T(8,128)(2,1)} fusion(bf16[1,8,1024,7168]{3,2,1,0:T(8,128)(2,1)} %bitcast.10, bf16[1,8,1024,7168]{3,2,1,0:T(8,128)(2,1)} %bitcast.9, bf16[1,8,1024,7168]{3,2,1,0:T(8,128)(2,1)} %bitcast.8), kind=kLoop, calls=%fused_computation.8 | loop fusion | flops 352321536 | bytes 704643072 | tf_op jit(solution)/shard_map/stack | solution.py:120
  2724.0 0.0 copy-done
  2724.0 0.0 copy-done.2
  2724.0 0.0 copy-done.3
  2724.0 359.8 %while.10 = (s32[]{:T(128)}, f32[3,8,1024,1024]{3,2,1,0:T(8,128)}, s32[3]{0:T(128)S(1)}, s32[3]{0:T(128)S(1)}, bf16[3,8,1024,7168]{3,2,1,0:T(8,128)(2,1)}, /*ind...) while((s32[]{:T(128)}, f32[3,8,1024,1024]{3,2,1,0:T(8,128)}, s32[3]{0:T(128)S(1)}, s32[3]{0:T(128)S(1)}, ...), condition=%wide.region_3.4_spmd, body=%wide.region_0.3_spmd.sunk | while | flops 120259084288 | bytes 335545120 | solution.py:138
  2724.0 0.6 dynamic_slice.63
  2725.2 0.0 copy-start.1
  2725.3 137.3 %conditional.2 = (f32[1,8,1024,1024]{3,2,1,0:T(8,128)}) conditional(s32[]{:T(128)} %bitcast.34, () %tuple.31, (s32[3]{0:T(128)S(1)}, s32[]{:T(128)}, bf16[3,8,1024,7168]{3,2,1,0:T(8,128)(2,1)}, s32[3]{0:T(128)S(1)}) %tuple.32), branch_computations={%region_1.1_spmd, %region_2.2_spmd} | conditional | flops 120259084288 | bytes 268435552 | solution.py:136
  2725.3 0.6 dynamic_slice.24
  2727.7 0.6 dynamic_slice.26
  2730.2 132.3 %fusion.5 = f32[1,8,1024,1024]{3,2,1,0:T(8,128)} fusion(bf16[3,8,1024,7168]{3,2,1,0:T(8,128)(2,1)} %get-tuple-element.55, s32[]{:T(128)S(6)} %select_n.12, s32[]{:T(128)S(6)} %select_n.11), kind=kOutput, calls=%fused_computation.5 | convolution fusion | flops 120259084288 | bytes 268435456 | tf_op jit(solution)/shard_map/while/body/eval_jaxpr/cond/branch_1_fun/lbk,lck->lbc/dot_general | solution.py:131
  2862.5 23.5 constant_dynamic-update-slice_fusion.2
  2886.0 0.0 copy-done.1
  2886.0 0.6 dynamic_slice.63
  2887.2 0.0 copy-start.1
  2887.2 137.2 %conditional.2 = (f32[1,8,1024,1024]{3,2,1,0:T(8,128)}) conditional(s32[]{:T(128)} %bitcast.34, () %tuple.31, (s32[3]{0:T(128)S(1)}, s32[]{:T(128)}, bf16[3,8,1024,7168]{3,2,1,0:T(8,128)(2,1)}, s32[3]{0:T(128)S(1)}) %tuple.32), branch_computations={%region_1.1_spmd, %region_2.2_spmd} | conditional | flops 120259084288 | bytes 268435552 | solution.py:136
  2887.2 0.6 dynamic_slice.24
  2889.7 0.6 dynamic_slice.26
  2892.1 132.3 %fusion.5 = f32[1,8,1024,1024]{3,2,1,0:T(8,128)} fusion(bf16[3,8,1024,7168]{3,2,1,0:T(8,128)(2,1)} %get-tuple-element.55, s32[]{:T(128)S(6)} %select_n.12, s32[]{:T(128)S(6)} %select_n.11), kind=kOutput, calls=%fused_computation.5 | convolution fusion | flops 120259084288 | bytes 268435456 | tf_op jit(solution)/shard_map/while/body/eval_jaxpr/cond/branch_1_fun/lbk,lck->lbc/dot_general | solution.py:131
  3024.4 23.5 constant_dynamic-update-slice_fusion.2
  3047.9 0.0 copy-done.1
  3047.9 0.6 dynamic_slice.63
  3049.1 0.0 copy-start.1
  3049.1 11.3 conditional.2
  3049.1 11.3 broadcast_in_dim.11
  3060.4 23.5 constant_dynamic-update-slice_fusion.2
  3083.8 0.0 copy-done.1
  3083.8 0.0 all-reduce.2.cloned.1.call-update
  3083.9 2334.1 %all-reduce.2.cloned.1.call-done = f32[1,3,8,1024,1024]{4,3,2,1,0:T(8,128)} async-done(((f32[1,3,8,1024,1024]{4,3,2,1,0:T(8,128)}), f32[1,3,8,1024,1024]{4,3,2,1,0:T(8,128)}) %all-reduce.2.cloned.1.call-update) | async-done | bytes 100663312 | tf_op jit(solution)/shard_map/psum | solution.py:139
  5417.9 65.8 %copy.17 = f32[1,3,8,1024,1024]{4,3,2,1,0:T(8,128)} copy(f32[1,3,8,1024,1024]{4,3,2,1,0:T(8,128)} %all-reduce.2.cloned.1.call-done) | data formatting | bytes 201326592
  (1 shorter events, 0.0 us)
Async XLA Ops:
  6.5 5411.4 %all-reduce.2.cloned.1.call-start = ((), (), s32[]{:S(2)}) async-start(), calls=%async_computation | async-start | bytes 201326592 | tf_op jit(solution)/shard_map/psum | solution.py:139
  6.5 2487.8 %collective-permute-start.1 = (bf16[8,1024,7168]{2,1,0:T(8,128)(2,1)}, bf16[8,1024,7168]{2,1,0:T(8,128)(2,1)}, u32[]{:S(2)}, u32[]{:S(2)}) collective-permute-start(bf16[8,1024,7168]{2,1,0:T(8,128)(2,1)} %param.8), channel_id=1, source_target_pairs={{0,1},{1,2},{4,5},{5,6}} | collective-permute-start | bytes 352321536 | tf_op jit(solution)/shard_map/ppermute | solution.py:119
  11.0 2483.3 %collective-permute-start = (bf16[8,1024,7168]{2,1,0:T(8,128)(2,1)}, bf16[8,1024,7168]{2,1,0:T(8,128)(2,1)}, u32[]{:S(2)}, u32[]{:S(2)}) collective-permute-start(bf16[8,1024,7168]{2,1,0:T(8,128)(2,1)} %param.8), channel_id=1, source_target_pairs={{0,2},{1,0},{2,3},{3,1},{4,6},{5,4},{6,7},{7,5}} | collective-permute-start | bytes 352321536 | tf_op jit(solution)/shard_map/ppermute | solution.py:119
  2494.3 229.6 %copy-start = (s32[3]{0:T(128)S(1)}, s32[3]{0:T(128)}, u32[]{:S(2)}) copy-start(s32[3]{0:T(128)} %get-tuple-element.121) | copy-start | bytes 40
  2494.3 229.6 %copy-start.2 = (s32[3]{0:T(128)S(1)}, s32[3]{0:T(128)}, u32[]{:S(2)}) copy-start(s32[3]{0:T(128)} %get-tuple-element.122) | copy-start | bytes 40
  2494.4 229.7 %copy-start.3 = (s32[3]{0:T(128)S(1)}, s32[3]{0:T(128)}, u32[]{:S(2)}) copy-start(s32[3]{0:T(128)} %fusion.13) | copy-start | bytes 40
  2725.2 160.7 %copy-start.1 = (s32[3]{0:T(128)S(1)}, s32[3]{0:T(128)}, u32[]{:S(2)}) copy-start(s32[3]{0:T(128)} %get-tuple-element.153) | copy-start | bytes 40 | tf_op jit(solution)/shard_map/while
  2887.2 160.7 %copy-start.1 = (s32[3]{0:T(128)S(1)}, s32[3]{0:T(128)}, u32[]{:S(2)}) copy-start(s32[3]{0:T(128)} %get-tuple-element.153) | copy-start | bytes 40 | tf_op jit(solution)/shard_map/while
  3049.1 34.7 copy-start.1
Sparse Core Ops, SparseCore 0:
  3084.0 2333.8 all-reduce.1
where the time goes:
time: 5490 us
  waiting for transfers between devices  4780 us (87%)
  matrix products  265 us (5%)
  other arithmetic  230 us (4%)
  local copies, waits for them, and re-layouts  154 us (3%)
    ppermute x2, waiting for transfers between devices, local_part(): received = [lax.ppermute(a_loc, 'g', round_pairs) for round_pairs in rounds]  2450 us
    psum x1, waiting for transfers between devices, local_part(): totals = lax.psum(partial_sums, 'kk')  2330 us
    dot_general x2, matrix products, compute(): jnp.einsum('lbk,lck->lbc', left_blk, right_blk, preferred_element_type=jn...  265 us
    another operation x1, other arithmetic, local_part(): held_blocks = jnp.stack([a_loc] + received, axis=0)  230 us
  transfers between devices with their start and end apart: 3, of which 2 were waited for; matrix products, arithmetic and copies ran while one was open for 0% of the time, Pallas kernels for 0%

commit v1 on v0

v1 whole, which is shorter than its diff:
```python
import functools

import jax
import jax.numpy as jnp
from jax import lax
from jax.experimental import pallas as pl
from jax.experimental.pallas import tpu as pltpu
from jax.sharding import PartitionSpec as P

MESH = pl.DeviceIdType.MESH
LANE = 128
AHEAD = 3
LEAD = 3


class Sizes:
    def __init__(self, layers, rows, cols):
        self.layers, self.rows, self.cols = layers, rows, cols
        self.half = layers // 2
        self.tile = rows // 2
        self.sub = self.tile // LANE
        self.full = self.sub * self.tile
        self.diag = self.sub * (self.sub + 1) // 2 * LANE
        self.own = 2 * self.diag + self.full
        self.mid = 4 * self.full
        self.part = 2 * self.full
        self.chunks = 2 * self.half
        self.depth = cols // 4 if cols % (4 * LANE) == 0 else cols


def exchange_kernel(sz, a, r, lp, rp, psd, psm, rsd, rsm, pc, rb, co, v, acc, stage, ba, bb,
                    load_sem, xs, xr, ls, lr, ds, dr, ss, sr, rss, rsr, cs, cr, fs):
    y = lax.axis_index("kk")
    g = lax.axis_index("g")
    x = g // 2
    c = g % 2
    away = c == x
    home = c != x
    layers, half, chunks = sz.layers, sz.half, sz.chunks

    to_x = {"g": (g + 2) % 4}
    to_core = {"g": 2 * x + 1 - c}
    to_y = {"kk": 1 - y}

    def remote(src, dst, send, recv, where):
        return pltpu.make_async_remote_copy(src_ref=src, dst_ref=dst, send_sem=send, recv_sem=recv, device_id=where,
                                            device_id_type=MESH)

    def x_in(q):
        j, h = q // 2, q % 2
        return remote(a.at[half * (1 - x) + j, h], r.at[j, h], xs.at[q], xr.at[q], to_x)

    def core_in(m):
        return remote(a.at[m], lp.at[m], ls.at[m], lr.at[m], to_core)

    def core_r(q):
        j, h = q // 2, q % 2
        return remote(r.at[j, h], rp.at[j, h], ds.at[q], dr.at[q], to_core)

    def send_diag(k, m):
        return remote(psd.at[k, m], rsd.at[k, m], ss.at[k, m], sr.at[k, m], to_y)

    def send_mid(m):
        return remote(psm.at[m], rsm.at[m], ss.at[2, m], sr.at[2, m], to_y)

    def send_part(q):
        src = pc.at[q, pl.ds(pl.multiple_of((1 - y) * sz.part, LANE), sz.part)]
        return remote(src, rb.at[q], rss.at[q], rsr.at[q], to_y)

    def send_sum(q):
        where = {"kk": jnp.where(home, 1 - y, y), "g": jnp.where(home, g, (g + 2) % 4)}
        return remote(co.at[x, q, y], co.at[x, q, y], cs.at[q], cr.at[jnp.where(home, 0, 1), q], where)

    def from_x(q):
        return remote(co.at[1 - x, q, y], co.at[1 - x, q, y], fs.at[q], cr.at[1, q], to_x)

    def forward(q):
        return remote(co.at[1 - x, q, y], co.at[1 - x, q, y], fs.at[q], cr.at[2, q], to_y)

    def load(src, dst, k):
        pltpu.make_async_copy(src, dst, load_sem.at[k]).start()

    def loaded(dst, k):
        pltpu.make_async_copy(dst, dst, load_sem.at[k]).wait()

    def store(src, dst):
        copy = pltpu.make_async_copy(src, dst, load_sem.at[6])
        copy.start()
        copy.wait()

    def product(left, right):
        acc[...] = jnp.zeros_like(acc)

        def step(k, carry):
            cols = pl.ds(pl.multiple_of(k * sz.depth, LANE), sz.depth)
            acc[...] += lax.dot_general(v[left, :, cols], v[right, :, cols], (((1,), (1,)), ((), ())),
                                        preferred_element_type=jnp.float32)
            return carry

        lax.fori_loop(0, sz.cols // sz.depth, step, 0)

    def put_full(row):
        for s in range(sz.sub):
            rows = pl.ds(pl.multiple_of(row + s * sz.tile, LANE), sz.tile)
            stage[rows, :] = acc[:, s * LANE:(s + 1) * LANE]

    def put_diag(row):
        n = 0
        for i in range(sz.sub):
            for k in range(i + 1):
                rows = pl.ds(pl.multiple_of(row + n * LANE, LANE), LANE)
                stage[rows, :] = acc[i * LANE:(i + 1) * LANE, k * LANE:(k + 1) * LANE]
                n += 1

    def same_chip(m):
        load(a.at[m, 0], v.at[0], 0)
        load(a.at[m, 1], v.at[1], 1)
        core_in(m).wait_recv()
        load(lp.at[m, 0], v.at[2], 2)
        load(lp.at[m, 1], v.at[3], 3)

        def diagonal(k):
            def one(d, carry):
                product(2 * k + d, 2 * k + d)
                put_diag(d * sz.diag)
                return carry

            lax.fori_loop(0, 2, one, 0)
            product(2 * k + 1, 2 * k)
            put_full(2 * sz.diag)
            store(stage.at[pl.ds(0, sz.own)], psd.at[k, m])
            send_diag(k, m).start()

        def middle(n, carry):
            i, k = n // 2, n % 2
            product(i + 2 * (1 - x), k + 2 * x)
            put_full(n * sz.full)
            return carry

        def diagonals(k, carry):
            for n in range(2):
                @pl.when(k == 0)
                def _():
                    loaded(v.at[n], n)
            diagonal(k)

            @pl.when(k == 0)
            def _():
                for n in range(2, 4):
                    loaded(v.at[n], n)
            return carry

        lax.fori_loop(0, 2, diagonals, 0)
        lax.fori_loop(0, 4, middle, 0)
        store(stage, psm.at[m])
        send_mid(m).start()

    def cross(q):
        j, h = q // 2, q % 2
        x_in(q).wait_recv()

        @pl.when(x == 0)
        def _():
            @pl.when(home & (h == 0))
            def _():
                core_in(j).wait_recv()

            own, other = 2 * c, 2 - 2 * c
            for n in range(2):
                load(a.at[j, n], v.at[own + n], n)
                load(lp.at[j, n], v.at[other + n], 2 + n)
            load(r.at[j, h], v.at[4], 4)
            for n in range(2):
                loaded(v.at[own + n], n)
                loaded(v.at[other + n], 2 + n)
            loaded(v.at[4], 4)

        @pl.when(x == 1)
        def _():
            core_r(q).start()
            for n in range(2):
                load(a.at[half + j, n], v.at[4 + n], n)
            load(r.at[j, h], v.at[c], 2)
            core_r(q).wait_recv()
            load(rp.at[j, h], v.at[1 - c], 3)
            for n in range(2):
                loaded(v.at[4 + n], n)
            loaded(v.at[c], 2)
            loaded(v.at[1 - c], 3)

        def one(n, carry):
            i, t = n // 2, n % 2
            product(4 + x * t, jnp.where(x == 0, n, i))
            put_full(n * sz.full)
            return carry

        lax.fori_loop(0, 4, one, 0)
        store(stage, pc.at[q])
        send_part(q).start()

    def add(q):
        send_part(q).wait_recv()
        load(pc.at[q, pl.ds(pl.multiple_of(y * sz.part, LANE), sz.part)], ba, 0)
        load(rb.at[q], bb, 1)
        loaded(ba, 0)
        loaded(bb, 1)
        ba[...] += bb[...]
        store(ba, co.at[x, q, y])
        send_sum(q).start()

    def pass_on(q):
        from_x(q).wait_recv()
        forward(q).start()

    barrier = pltpu.get_barrier_semaphore()
    for where in (to_x, to_core, to_y):
        pl.semaphore_signal(barrier, inc=1, device_id=where, device_id_type=MESH)
    pl.semaphore_wait(barrier, 3)

    def loop(lo, hi, f):
        def body(n, carry):
            f(n)
            return carry

        lax.fori_loop(lo, hi, body, 0)

    loop(0, AHEAD, lambda q: x_in(q).start())

    @pl.when(home)
    def _():
        loop(0, layers, lambda m: core_in(m).start())

    @pl.when(away & (x == 0))
    def _():
        loop(0, half, lambda m: core_in(m).start())

    @pl.when(away)
    def _():
        loop(0, LEAD, same_chip)

    def round_(q):
        cross(q)

        @pl.when(away & (q < layers - LEAD))
        def _():
            same_chip(q + LEAD)

        add(q)

        @pl.when(q < chunks - AHEAD)
        def _():
            x_in(q + AHEAD).start()

        @pl.when(home & (q >= 2))
        def _():
            pass_on(q - 2)

    loop(0, chunks, round_)

    @pl.when(home)
    def _():
        loop(chunks - 2, chunks, pass_on)
        loop(0, layers, lambda m: core_in(m).wait_send())

        def end(q):
            send_sum(q).wait_recv()
            forward(q).wait_recv()
            forward(q).wait_send()

        loop(0, chunks, end)

    @pl.when(away & (x == 0))
    def _():
        loop(0, half, lambda m: core_in(m).wait_send())

    @pl.when(x == 1)
    def _():
        loop(0, chunks, lambda q: core_r(q).wait_send())

    @pl.when(away)
    def _():
        def end(m):
            for k in range(2):
                send_diag(k, m).wait()
            send_mid(m).wait()

        loop(0, layers, end)

    def sent(q):
        x_in(q).wait_send()
        send_part(q).wait_send()
        send_sum(q).wait_send()

    loop(0, chunks, sent)


def exchange(sz, a):
    f32, bf16 = jnp.float32, jnp.bfloat16
    dma = pltpu.SemaphoreType.DMA
    halves = (2, sz.tile, sz.cols)
    outs = [
        ((sz.half,) + halves, bf16),
        ((sz.layers,) + halves, bf16),
        ((sz.half,) + halves, bf16),
        ((2, sz.layers, sz.own, LANE), f32),
        ((sz.layers, sz.mid, LANE), f32),
        ((2, sz.layers, sz.own, LANE), f32),
        ((sz.layers, sz.mid, LANE), f32),
        ((sz.chunks, 2 * sz.part, LANE), f32),
        ((sz.chunks, sz.part, LANE), f32),
        ((2, sz.chunks, 2, sz.part, LANE), f32),
    ]
    n, q = sz.layers, sz.chunks
    res = pl.pallas_call(
        functools.partial(exchange_kernel, sz),
        name="exchange",
        out_shape=[jax.ShapeDtypeStruct(s, d) for s, d in outs],
        in_specs=[pl.BlockSpec(memory_space=pl.ANY)],
        out_specs=[pl.BlockSpec(memory_space=pl.ANY)] * len(outs),
        scratch_shapes=[
            pltpu.VMEM((6, sz.tile, sz.cols), bf16),
            pltpu.VMEM((sz.tile, sz.tile), f32),
            pltpu.VMEM((sz.mid, LANE), f32),
            pltpu.VMEM((sz.part, LANE), f32),
            pltpu.VMEM((sz.part, LANE), f32),
            dma((7,)), dma((q,)), dma((q,)), dma((n,)), dma((n,)), dma((q,)), dma((q,)),
            dma((3, n)), dma((3, n)), dma((q,)), dma((q,)), dma((q,)), dma((3, q)), dma((q,)),
        ],
        compiler_params=pltpu.CompilerParams(collective_id=0, has_side_effects=True, vmem_limit_bytes=60 * 2**20),
    )(a)
    return res[3], res[5], res[4], res[6], res[9]


def assemble_kernel(sz, role, psd0, rsd0, psm, rsm, psd1, rsd1, co, out):
    away = role[0] == 1
    x = role[1]
    t, sub = sz.tile, sz.sub
    slot = pl.program_id(1)
    m = pl.program_id(0)

    def diagonal(mine, theirs):
        for d in range(2):
            n = 0
            for i in range(sub):
                for k in range(i + 1):
                    rows = slice(d * sz.diag + n * LANE, d * sz.diag + (n + 1) * LANE)
                    s = mine[0, 0, rows, :] + theirs[0, 0, rows, :]
                    lo, hi = d * t + i * LANE, d * t + k * LANE
                    out[0, 0, lo:lo + LANE, hi:hi + LANE] = s
                    if i != k:
                        out[0, 0, hi:hi + LANE, lo:lo + LANE] = s.T
                    n += 1
        for k in range(sub):
            for i in range(sub):
                rows = slice(2 * sz.diag + k * t + i * LANE, 2 * sz.diag + k * t + (i + 1) * LANE)
                s = mine[0, 0, rows, :] + theirs[0, 0, rows, :]
                lo, hi = t + i * LANE, k * LANE
                out[0, 0, lo:lo + LANE, hi:hi + LANE] = s
                out[0, 0, hi:hi + LANE, lo:lo + LANE] = s.T

    @pl.when(away & (slot == 2 * x))
    def _():
        diagonal(psd0, rsd0)

    @pl.when(away & (slot == 2 - 2 * x))
    def _():
        diagonal(psd1, rsd1)

    @pl.when(away & (slot == 1))
    def _():
        for n in range(4):
            i, k = n // 2, n % 2
            for s in range(sub):
                rows = slice(n * sz.full + s * t, n * sz.full + (s + 1) * t)
                col = k * t + s * LANE
                out[0, 0, i * t:(i + 1) * t, col:col + LANE] = psm[0, rows, :] + rsm[0, rows, :]

    def cross(first):
        for h in range(2):
            for n in range(2):
                i, k = (h, n) if first else (n, h)
                for s in range(sub):
                    rows = slice(n * sz.full + s * t, n * sz.full + (s + 1) * t)
                    col = k * t + s * LANE
                    out[0, 0, i * t:(i + 1) * t, col:col + LANE] = co[0, h, 0, rows, :]

    @pl.when((role[0] == 0) & (slot < 2) & (m < sz.half))
    def _():
        cross(True)

    @pl.when((role[0] == 0) & (slot < 2) & (m >= sz.half))
    def _():
        cross(False)

    @pl.when((role[0] == 0) & (slot == 2))
    def _():
        out[...] = jnp.zeros_like(out)


def assemble(sz, role, psd, rsd, psm, rsm, co):
    def diag_at(k):
        return lambda m, slot, role: (k, m * role[0], 0, 0)

    def mid_at(m, slot, role):
        return (m * role[0], 0, 0)

    def cross_at(m, slot, role):
        home = 1 - role[0]
        return (home * (m // sz.half), home * (m % sz.half), home * jnp.minimum(slot, 1), 0, 0)

    diag = (1, 1, sz.own, LANE)
    mid = (1, sz.mid, LANE)
    return pl.pallas_call(
        functools.partial(assemble_kernel, sz),
        name="assemble",
        out_shape=jax.ShapeDtypeStruct((3, sz.layers, sz.rows, sz.rows), jnp.float32),
        grid_spec=pltpu.PrefetchScalarGridSpec(
            num_scalar_prefetch=1,
            grid=(sz.layers, 3),
            in_specs=[
                pl.BlockSpec(diag, diag_at(0)), pl.BlockSpec(diag, diag_at(0)),
                pl.BlockSpec(mid, mid_at), pl.BlockSpec(mid, mid_at),
                pl.BlockSpec(diag, diag_at(1)), pl.BlockSpec(diag, diag_at(1)),
                pl.BlockSpec((1, 2, 1, sz.part, LANE), cross_at),
            ],
            out_specs=pl.BlockSpec((1, 1, sz.rows, sz.rows), lambda m, slot, role: (slot, m, 0, 0)),
        ),
        compiler_params=pltpu.CompilerParams(vmem_limit_bytes=60 * 2**20),
    )(role, psd, rsd, psm, rsm, psd, rsd, co)


def solution(mesh):
    def local_part(a_loc):
        sz = Sizes(*a_loc.shape)
        g = lax.axis_index("g")
        x, c = g // 2, g % 2
        role = jnp.stack([jnp.where(c == x, 1, 0), x]).astype(jnp.int32)
        parts = exchange(sz, a_loc.reshape(sz.layers, 2, sz.tile, sz.cols))
        return assemble(sz, role, *parts)[None]

    return jax.shard_map(local_part, mesh=mesh, in_specs=(P(None, ("m", "g"), "kk"),), out_specs=P(("m", "g"), None, None, None, None), check_vma=False)
```

time: 5490 us -> 1640 us (0.30)
  waiting for transfers between devices: 4780 us -> 0 us
  Pallas kernels: 0 us -> 1610 us
  matrix products: 265 us -> 0 us
  other arithmetic: 230 us -> 0.58 us
  local copies, waits for them, and re-layouts: 154 us -> 0 us
    ppermute x2 -> x0, waiting for transfers between devices: 2450 us -> none  [local_part(): received = [lax.ppermute(a_loc, 'g', round_pairs) for round_pairs in rounds]]
    psum x1 -> x0, waiting for transfers between devices: 2330 us -> none  [local_part(): totals = lax.psum(partial_sums, 'kk')]
    pallas_call x0 -> x2, Pallas kernels: none -> 1610 us  [the longest x1 1550 us: exchange(): pl.pallas_call(functools.partial(exchange_kernel, sz), name='exchange', o...]
    dot_general x2 -> x0, matrix products: 265 us -> none  [compute(): jnp.einsum('lbk,lck->lbc', left_blk, right_blk, preferred_element_type=jn...]
    another operation x1, other arithmetic: 230 us -> 0.58 us  [local_part(): role = jnp.stack([jnp.where(c == x, 1, 0), x]).astype(jnp.int32)]
    dynamic_update_slice x3 -> x0, local copies, waits for them, and re-layouts: 70.4 us -> none  [local_part(): partial_sums = lax.map(one_slot, (left_slots, right_slots, live_slots))]
    unnamed x7 -> x0, local copies, waits for them, and re-layouts: 65.8 us -> none
  transfers between devices with their start and end apart: 3 -> 0, of which waited for: 2 -> 0; matrix products, arithmetic and copies ran while one was open for 0% -> 0% of each run, Pallas kernels for 0% -> 0%
where the time goes in v1:
time: 1640 us; the launch traced here: 1610 us
  Pallas kernels  1610 us (98%)
    pallas_call x1, Pallas kernels, exchange(): pl.pallas_call(functools.partial(exchange_kernel, sz), name='exchange', o...  1550 us
    pallas_call x1, Pallas kernels, assemble(): pl.pallas_call(functools.partial(assemble_kernel, sz), name='assemble', o...  61.4 us

profile of v1, /device:TPU:1, one launch (start us, length us, event | category | flops | bytes accessed | tf_op | source)
XLA Modules:
  0.0 1607.5 jit_solution(62326748487110783)
XLA Ops:
  0.0 0.6 pad_add_fusion.role
  0.6 1545.5 %exchange.1 = (bf16[4,2,512,7168]{3,2,1,0:T(8,128)(2,1)}, bf16[8,2,512,7168]{3,2,1,0:T(8,128)(2,1)}, bf16[4,2,512,7168]{3,2,1,0:T(8,128)(2,1)}, f32[2,8,4608,128...) custom-call(bf16[8,2,512,7168]{3,2,1,0:T(8,128)(2,1)} %bitcast.2.a), custom_call_target="tpu_custom_call" | custom-call | tf_op jit(solution)/shard_map/exchange/pallas_call | solution.py:314
  1546.1 61.4 %assemble.1 = f32[3,8,1024,1024]{3,2,1,0:T(8,128)} custom-call(s32[2]{0:T(128)} %pad_add_fusion.role, f32[2,8,4608,128]{3,2,1,0:T(8,128)} %get-tuple-element.10.psd0.psd1, f32[2,8,4608,128]{3,2,1,0:T(8,128)} %get-tuple-element.11.rsd0.rsd1, f32[8,8192,128]{2,1,0:T(8,128)} %get-tuple-element.12.psm, f32[8,8192,128]{2,1,0:T(8,128)} %get-tuple-element.13.rsm, ...), custom_call_target="tpu_custom_call" | custom-call | tf_op jit(solution)/shard_map/assemble/pallas_call | solution.py:413

commit v2 on v1

v2 whole, which is shorter than its diff:
```python
import functools

import jax
import jax.numpy as jnp
from jax import lax
from jax.experimental import pallas as pl
from jax.experimental.pallas import tpu as pltpu
from jax.sharding import PartitionSpec as P

MESH = pl.DeviceIdType.MESH
LANE = 128
CHUNKS = 4

PLAN = (
    (
        "SISIXSAISISXXIISSASXSSXISASSXIAXISAAXAXIXISSISAISS",
        "SISXXSXSIAXAAXAAISXAAA",
    ),
    (
        "IIXIIXIXXAIFAIXAFIAXIIAXAXIIAIXIXFFXAFXFAAAIAXFIFF",
        "XAXAFFAFXFFFFA",
    ),
    (
        "IIRIRXIAIXIRIRAXIRRXXFFAIAAIIXRRRFIFRIAXIAFFIXRRAX",
        "AXXRFFIAAXRRAXFFXFXAFAAFRFXFAF",
    ),
    (
        "SSSISRSISRXSASSIXASRXRISRISAXSIAISXSISRIXAISSRIIIX",
        "ASRSXRSRSXSXASAAIRAIIXRRXXRARXAXAARAXA",
    ),
)
STEPS = "IRXAFS"
WORD = 10


def plan_words():
    rows = []
    for pieces in PLAN:
        codes, count, kept = [], 0, False
        for step in "".join(pieces):
            codes.append(STEPS.index(step) + 1)
            if step == "S":
                codes[-1] += kept and count % 3 > 0
                count, kept = count + 1, True
            kept = kept and step != "X"
        rows.append([sum(code << (3 * k) for k, code in enumerate(codes[n:n + WORD])) for n in range(0, len(codes), WORD)])
    longest = max(len(row) for row in rows)
    return [row + [0] * (longest - len(row)) for row in rows]


class Sizes:
    def __init__(self, layers, rows, cols):
        self.layers, self.rows, self.cols = layers, rows, cols
        self.half = layers // 2
        self.tile = rows // 2
        self.piece = rows // CHUNKS
        self.sub = self.tile // LANE
        self.full = self.sub * self.tile
        self.pairs = (self.sub + 1) // 2
        self.low = self.sub * (self.sub - 1) // 2
        self.diag = (self.low + self.pairs) * LANE + (self.pairs + 7) // 8 * 8
        self.own = 2 * self.diag + self.full
        self.mid = 4 * self.full
        self.flat = self.piece // LANE * self.tile
        self.part = 2 * self.flat
        self.chunks = CHUNKS * self.half
        self.depth = cols // 4 if cols % (4 * LANE) == 0 else cols


def triangles():
    row = lax.broadcasted_iota(jnp.int32, (LANE, LANE), 0)
    col = lax.broadcasted_iota(jnp.int32, (LANE, LANE), 1)
    return row >= col, row == col


def exchange_kernel(sz, a, r, lp, rp, psd, psm, rsd, rsm, pc, rb, co, v, acc, stage, ba, bb,
                    load_sem, xs, xr, ls, lr, ds, dr, ss, sr, rss, rsr, cs, cr, fs):
    y = lax.axis_index("kk")
    g = lax.axis_index("g")
    x = g // 2
    c = g % 2
    away = c == x
    home = c != x
    layers, half, chunks = sz.layers, sz.half, sz.chunks

    to_x = {"g": (g + 2) % 4}
    to_core = {"g": 2 * x + 1 - c}
    to_y = {"kk": 1 - y}

    def remote(src, dst, send, recv, where):
        return pltpu.make_async_remote_copy(src_ref=src, dst_ref=dst, send_sem=send, recv_sem=recv, device_id=where,
                                            device_id_type=MESH)

    def chunk(ref, q):
        return ref.at[q // CHUNKS, pl.ds(pl.multiple_of(q % CHUNKS * sz.piece, sz.piece), sz.piece)]

    def x_in(q):
        return remote(chunk(a, half * (1 - x) * CHUNKS + q), chunk(r, q), xs.at[q], xr.at[q], to_x)

    def core_in(m):
        return remote(a.at[m], lp.at[m], ls.at[m], lr.at[m], to_core)

    def core_r(q):
        return remote(chunk(r, q), chunk(rp, q), ds.at[q], dr.at[q], to_core)

    def send_diag(k, m, rows=None):
        src, dst = psd.at[k, m], rsd.at[k, m]
        if rows is not None:
            src, dst = src.at[rows], dst.at[rows]
        return remote(src, dst, ss.at[k, m], sr.at[k, m], to_y)

    def send_mid(m, rows=None):
        src, dst = psm.at[m], rsm.at[m]
        if rows is not None:
            src, dst = src.at[rows], dst.at[rows]
        return remote(src, dst, ss.at[2, m], sr.at[2, m], to_y)

    def send_part(q):
        src = pc.at[q, pl.ds(pl.multiple_of((1 - y) * sz.part, LANE), sz.part)]
        return remote(src, rb.at[q], rss.at[q], rsr.at[q], to_y)

    def send_sum(q):
        where = {"kk": jnp.where(home, 1 - y, y), "g": jnp.where(home, g, (g + 2) % 4)}
        return remote(co.at[x, q, y], co.at[x, q, y], cs.at[q], cr.at[jnp.where(home, 0, 1), q], where)

    def from_x(q):
        return remote(co.at[1 - x, q, y], co.at[1 - x, q, y], fs.at[q], cr.at[1, q], to_x)

    def forward(q):
        return remote(co.at[1 - x, q, y], co.at[1 - x, q, y], fs.at[q], cr.at[2, q], to_y)

    def load(src, dst, k):
        pltpu.make_async_copy(src, dst, load_sem.at[k]).start()

    def loaded(dst, k):
        pltpu.make_async_copy(dst, dst, load_sem.at[k]).wait()

    def store(src, dst):
        copy = pltpu.make_async_copy(src, dst, load_sem.at[4])
        copy.start()
        copy.wait()

    def block(n, rows=sz.rows):
        return v.at[pl.ds(pl.multiple_of(n, LANE), rows)]

    def product(left, right, width):
        acc[:, :width] = jnp.zeros((sz.tile, width), jnp.float32)

        def step(k, carry):
            cols = pl.ds(pl.multiple_of(k * sz.depth, LANE), sz.depth)
            lhs = v[pl.ds(pl.multiple_of(left, LANE), sz.tile), cols]
            rhs = v[pl.ds(pl.multiple_of(right, LANE), width), cols]
            acc[:, :width] += lax.dot_general(lhs, rhs, (((1,), (1,)), ((), ())), preferred_element_type=jnp.float32)
            return carry

        lax.fori_loop(0, sz.cols // sz.depth, step, 0)

    def put_strips(row, width):
        for s in range(width // LANE):
            rows = pl.ds(pl.multiple_of(row + s * sz.tile, 8), sz.tile)
            stage[rows, :] = acc[:, s * LANE:(s + 1) * LANE]

    def put_diag(row):
        def subtile(i, k):
            return acc[i * LANE:(i + 1) * LANE, k * LANE:(k + 1) * LANE]

        n = row
        for i in range(sz.sub):
            for k in range(i):
                stage[n:n + LANE, :] = subtile(i, k)
                n += LANE
        lower, equal = triangles()
        tail = row + (sz.low + sz.pairs) * LANE
        stage[tail:row + sz.diag, :] = jnp.zeros((row + sz.diag - tail, LANE), jnp.float32)
        for i in range(0, sz.sub, 2):
            if i + 1 < sz.sub:
                other = subtile(i + 1, i + 1)
                stage[n:n + LANE, :] = jnp.where(lower, subtile(i, i), other)
                stage[tail + i // 2:tail + i // 2 + 1, :] = jnp.sum(jnp.where(equal, other, 0.0), axis=0, keepdims=True)
            else:
                stage[n:n + LANE, :] = subtile(i, i)
            n += LANE

    def same_chip(n, kept):
        m, k = n // 3, n % 3

        def halves(ref, at):
            for d in range(2):
                load(ref.at[m, pl.ds(d * sz.tile, sz.tile)], block(at + d * sz.tile, sz.tile), d)

        @pl.when(k == 0)
        def _():
            halves(a, 0)

        @pl.when((k == 2) & (kept == 0))
        def _():
            halves(lp, sz.rows)

        @pl.when(k == 1)
        def _():
            core_in(m).wait_recv()

            @pl.when(kept == 0)
            def _():
                load(a.at[m], block(0), 2)
                loaded(block(0), 2)

            load(lp.at[m], block(sz.rows), 3)
            loaded(block(sz.rows), 3)

            def middle(i, carry):
                lhs, rhs = i // 2 * sz.tile + (1 - x) * sz.rows, i % 2 * sz.tile + x * sz.rows
                product(lhs, rhs, sz.tile)
                put_strips(i * sz.full, sz.tile)

                @pl.when(n == 1)
                def _():
                    rows = pl.ds(pl.multiple_of(i * sz.full, LANE), sz.full)
                    store(stage.at[rows], psm.at[m, rows])
                    send_mid(m, rows).start()
                return carry

            lax.fori_loop(0, 4, middle, 0)

            @pl.when(n > 1)
            def _():
                store(stage, psm.at[m])
                send_mid(m).start()

        @pl.when(k != 1)
        def _():
            which = k // 2
            base = which * sz.rows

            def piece(lo, size):
                @pl.when(n == 0)
                def _():
                    rows = pl.ds(lo, size)
                    store(stage.at[rows], psd.at[which, m, rows])
                    send_diag(which, m, rows).start()

            for d in range(2):
                @pl.when((k == 0) | (kept == 0))
                def _():
                    loaded(block(base + d * sz.tile, sz.tile), d)

                product(base + d * sz.tile, base + d * sz.tile, sz.tile)
                put_diag(d * sz.diag)
                piece(d * sz.diag, sz.diag)
            product(base + sz.tile, base, sz.tile)
            put_strips(2 * sz.diag, sz.tile)
            piece(2 * sz.diag, sz.full)

            @pl.when(n > 0)
            def _():
                store(stage.at[pl.ds(0, sz.own)], psd.at[which, m])
                send_diag(which, m).start()

    def relay(q):
        x_in(q).wait_recv()
        core_r(q).start()

    def cross(q):
        j = q // CHUNKS

        @pl.when(x == 0)
        def _():
            @pl.when(home & (q % CHUNKS == 0))
            def _():
                core_in(j).wait_recv()

            load(a.at[j], block(c * sz.rows), 0)
            load(lp.at[j], block((1 - c) * sz.rows), 1)
            x_in(q).wait_recv()
            load(chunk(r, q), block(2 * sz.rows, sz.piece), 2)
            loaded(block(c * sz.rows), 0)
            loaded(block((1 - c) * sz.rows), 1)
            loaded(block(2 * sz.rows, sz.piece), 2)

        @pl.when(x == 1)
        def _():
            load(a.at[half + j], block(2 * sz.rows), 0)
            load(chunk(r, q), block(c * sz.piece, sz.piece), 1)
            core_r(q).wait_recv()
            load(chunk(rp, q), block((1 - c) * sz.piece, sz.piece), 2)
            loaded(block(2 * sz.rows), 0)
            loaded(block(c * sz.piece, sz.piece), 1)
            loaded(block((1 - c) * sz.piece, sz.piece), 2)

        def one(n, carry):
            lhs = n * sz.tile * (1 - x) + (2 * sz.rows + n % 2 * sz.tile) * x
            rhs = 2 * sz.rows * (1 - x) + n // 2 * sz.piece * x
            product(lhs, rhs, sz.piece)
            put_strips(n * sz.flat, sz.piece)
            return carry

        lax.fori_loop(0, 4, one, 0)
        store(stage.at[pl.ds(0, 2 * sz.part)], pc.at[q])
        send_part(q).start()

    def add(q):
        load(pc.at[q, pl.ds(pl.multiple_of(y * sz.part, LANE), sz.part)], ba, 0)
        send_part(q).wait_recv()
        load(rb.at[q], bb, 1)
        loaded(ba, 0)
        loaded(bb, 1)
        ba[...] += bb[...]
        store(ba, co.at[x, q, y])
        send_sum(q).start()

    def pass_on(q):
        from_x(q).wait_recv()
        forward(q).start()

    barrier = pltpu.get_barrier_semaphore()
    for where in (to_x, to_core, to_y):
        pl.semaphore_signal(barrier, inc=1, device_id=where, device_id_type=MESH)
    pl.semaphore_wait(barrier, 3)

    def loop(lo, hi, f):
        def body(n, carry):
            f(n)
            return carry

        lax.fori_loop(lo, hi, body, 0)

    @pl.when(home)
    def _():
        loop(0, layers, lambda m: core_in(m).start())

    @pl.when(away & (x == 0))
    def _():
        loop(0, half, lambda m: core_in(m).start())

    steps = [lambda q: x_in(q).start(), relay, cross, add, pass_on]

    def word(n, done):
        code = jnp.int32(0)
        for device, words in enumerate(plan_words()):
            for k, value in enumerate(words):
                code = jnp.where((g == device) & (n == k), value, code)

        def digit(_, carry):
            code, done = carry[0], list(carry[1:])
            now = code % 8
            for k, step in enumerate(steps):
                pl.when(now == k + 1)(functools.partial(step, done[k]))
                done[k] += jnp.where(now == k + 1, 1, 0)
            pl.when(now > len(steps))(functools.partial(same_chip, done[-1], now - len(steps) - 1))
            done[-1] += jnp.where(now > len(steps), 1, 0)
            return (code // 8, *done)

        return lax.fori_loop(0, WORD, digit, (code, *done))[1:]

    lax.fori_loop(0, len(plan_words()[0]), word, (jnp.int32(0),) * (len(steps) + 1))

    @pl.when(home)
    def _():
        loop(0, layers, lambda m: core_in(m).wait_send())

        def end(q):
            send_sum(q).wait_recv()
            forward(q).wait_recv()
            forward(q).wait_send()

        loop(0, chunks, end)

    @pl.when(away & (x == 0))
    def _():
        loop(0, half, lambda m: core_in(m).wait_send())

    @pl.when(x == 1)
    def _():
        loop(0, chunks, lambda q: core_r(q).wait_send())

    @pl.when(away)
    def _():
        def end(m):
            for k in range(2):
                send_diag(k, m).wait()
            send_mid(m).wait()

        loop(0, layers, end)

    def sent(q):
        x_in(q).wait_send()
        send_part(q).wait_send()
        send_sum(q).wait_send()

    loop(0, chunks, sent)


def exchange(sz, a):
    f32, bf16 = jnp.float32, jnp.bfloat16
    dma = pltpu.SemaphoreType.DMA
    rows = (sz.rows, sz.cols)
    outs = [
        ((sz.half,) + rows, bf16),
        ((sz.layers,) + rows, bf16),
        ((sz.half,) + rows, bf16),
        ((2, sz.layers, sz.own, LANE), f32),
        ((sz.layers, sz.mid, LANE), f32),
        ((2, sz.layers, sz.own, LANE), f32),
        ((sz.layers, sz.mid, LANE), f32),
        ((sz.chunks, 2 * sz.part, LANE), f32),
        ((sz.chunks, sz.part, LANE), f32),
        ((2, sz.chunks, 2, sz.part, LANE), f32),
    ]
    n, q = sz.layers, sz.chunks
    res = pl.pallas_call(
        functools.partial(exchange_kernel, sz),
        name="exchange",
        out_shape=[jax.ShapeDtypeStruct(s, d) for s, d in outs],
        in_specs=[pl.BlockSpec(memory_space=pl.ANY)],
        out_specs=[pl.BlockSpec(memory_space=pl.ANY)] * len(outs),
        scratch_shapes=[
            pltpu.VMEM((3 * sz.rows, sz.cols), bf16),
            pltpu.VMEM((sz.tile, sz.tile), f32),
            pltpu.VMEM((sz.mid, LANE), f32),
            pltpu.VMEM((sz.part, LANE), f32),
            pltpu.VMEM((sz.part, LANE), f32),
            dma((5,)), dma((q,)), dma((q,)), dma((n,)), dma((n,)), dma((q,)), dma((q,)),
            dma((3, n)), dma((3, n)), dma((q,)), dma((q,)), dma((q,)), dma((3, q)), dma((q,)),
        ],
        compiler_params=pltpu.CompilerParams(collective_id=0, has_side_effects=True, vmem_limit_bytes=60 * 2**20),
    )(a)
    return res[3], res[5], res[4], res[6], res[9]


def assemble_kernel(sz, role, psd0, rsd0, psm, rsm, psd1, rsd1, co, out):
    away = role[0] == 1
    x = role[1]
    t, sub = sz.tile, sz.sub
    slot = pl.program_id(1)
    m = pl.program_id(0)

    lower, equal = triangles()

    def put(i, k, value):
        out[0, 0, i * LANE:(i + 1) * LANE, k * LANE:(k + 1) * LANE] = value

    def diagonal(mine, theirs):
        def total(row, size=LANE):
            return mine[0, 0, row:row + size, :] + theirs[0, 0, row:row + size, :]

        for d in range(2):
            row, first = d * sz.diag, d * sub
            tail = row + (sz.low + sz.pairs) * LANE
            for i in range(sub):
                for k in range(i):
                    s = total(row)
                    put(first + i, first + k, s)
                    put(first + k, first + i, s.T)
                    row += LANE
            for i in range(0, sub, 2):
                s = total(row)
                flip = s.T
                put(first + i, first + i, jnp.where(lower, s, flip))
                if i + 1 < sub:
                    line = jnp.broadcast_to(total(tail + i // 2, 1), (LANE, LANE))
                    other = jnp.where(equal, line, jnp.where(lower, flip, s))
                    put(first + i + 1, first + i + 1, other)
                row += LANE
        for k in range(sub):
            for i in range(sub):
                s = total(2 * sz.diag + k * t + i * LANE)
                put(sub + i, k, s)
                put(k, sub + i, s.T)

    @pl.when(away & (slot == 2 * x))
    def _():
        diagonal(psd0, rsd0)

    @pl.when(away & (slot == 2 - 2 * x))
    def _():
        diagonal(psd1, rsd1)

    @pl.when(away & (slot == 1))
    def _():
        for n in range(4):
            i, k = n // 2, n % 2
            for s in range(sub):
                rows = slice(n * sz.full + s * t, n * sz.full + (s + 1) * t)
                col = k * t + s * LANE
                out[0, 0, i * t:(i + 1) * t, col:col + LANE] = psm[0, rows, :] + rsm[0, rows, :]

    def cross(transposed):
        strips = sz.piece // LANE
        for h in range(CHUNKS):
            for n in range(2):
                for s in range(strips):
                    for i in range(sub):
                        row = n * sz.flat + s * t + i * LANE
                        value = co[0, h, 0, row:row + LANE, :]
                        across, along = h * strips + s, n * sub + i
                        if transposed:
                            put(across, along, value.T)
                        else:
                            put(along, across, value)

    @pl.when((role[0] == 0) & (slot < 2) & (m < sz.half))
    def _():
        cross(True)

    @pl.when((role[0] == 0) & (slot < 2) & (m >= sz.half))
    def _():
        cross(False)

    @pl.when((role[0] == 0) & (slot == 2))
    def _():
        out[...] = jnp.zeros_like(out)


def assemble(sz, role, psd, rsd, psm, rsm, co):
    def diag_at(k):
        return lambda m, slot, role: (k, m * role[0], 0, 0)

    def mid_at(m, slot, role):
        return (m * role[0], 0, 0)

    def cross_at(m, slot, role):
        home = 1 - role[0]
        return (home * (m // sz.half), home * (m % sz.half), home * jnp.minimum(slot, 1), 0, 0)

    diag = (1, 1, sz.own, LANE)
    mid = (1, sz.mid, LANE)
    return pl.pallas_call(
        functools.partial(assemble_kernel, sz),
        name="assemble",
        out_shape=jax.ShapeDtypeStruct((3, sz.layers, sz.rows, sz.rows), jnp.float32),
        grid_spec=pltpu.PrefetchScalarGridSpec(
            num_scalar_prefetch=1,
            grid=(sz.layers, 3),
            in_specs=[
                pl.BlockSpec(diag, diag_at(0)), pl.BlockSpec(diag, diag_at(0)),
                pl.BlockSpec(mid, mid_at), pl.BlockSpec(mid, mid_at),
                pl.BlockSpec(diag, diag_at(1)), pl.BlockSpec(diag, diag_at(1)),
                pl.BlockSpec((1, CHUNKS, 1, sz.part, LANE), cross_at),
            ],
            out_specs=pl.BlockSpec((1, 1, sz.rows, sz.rows), lambda m, slot, role: (slot, m, 0, 0)),
        ),
        compiler_params=pltpu.CompilerParams(vmem_limit_bytes=60 * 2**20),
    )(role, psd, rsd, psm, rsm, psd, rsd, co)


def solution(mesh):
    def local_part(a_loc):
        sz = Sizes(*a_loc.shape)
        g = lax.axis_index("g")
        x, c = g // 2, g % 2
        role = jnp.stack([jnp.where(c == x, 1, 0), x]).astype(jnp.int32)
        parts = exchange(sz, a_loc)
        return assemble(sz, role, *parts)[None]

    return jax.shard_map(local_part, mesh=mesh, in_specs=(P(None, ("m", "g"), "kk"),), out_specs=P(("m", "g"), None, None, None, None), check_vma=False)
```

time: 1640 us -> 1560 us (0.951); the launches traced: 1610 us -> 1560 us
  Pallas kernels: 1610 us -> 1560 us
    pallas_call x1, Pallas kernels: 1550 us -> 1500 us  [exchange(): pl.pallas_call(functools.partial(exchange_kernel, sz), name='exchange', o...]
where the time goes in v2:
time: 1560 us
  Pallas kernels  1560 us (100%)
    pallas_call x1, Pallas kernels, exchange(): pl.pallas_call(functools.partial(exchange_kernel, sz), name='exchange', o...  1500 us
    pallas_call x1, Pallas kernels, assemble(): pl.pallas_call(functools.partial(assemble_kernel, sz), name='assemble', o...  63.8 us

profile of v2, /device:TPU:1, one launch (start us, length us, event | category | flops | bytes accessed | tf_op | source)
XLA Modules:
  0.0 1559.6 jit_solution(314710602117308088)
XLA Ops:
  0.0 0.6 pad_add_fusion.role
  0.6 1495.2 %exchange.1 = (bf16[4,1024,7168]{2,1,0:T(8,128)(2,1)}, bf16[8,1024,7168]{2,1,0:T(8,128)(2,1)}, bf16[4,1024,7168]{2,1,0:T(8,128)(2,1)}, f32[2,8,4112,128]{3,2,1,0...) custom-call(bf16[8,1024,7168]{2,1,0:T(8,128)(2,1)} %a.1), custom_call_target="tpu_custom_call" | custom-call | tf_op jit(solution)/shard_map/exchange/pallas_call | solution.py:410
  1495.8 63.8 %assemble.1 = f32[3,8,1024,1024]{3,2,1,0:T(8,128)} custom-call(s32[2]{0:T(128)} %pad_add_fusion.role, f32[2,8,4112,128]{3,2,1,0:T(8,128)} %get-tuple-element.10.psd0.psd1, f32[2,8,4112,128]{3,2,1,0:T(8,128)} %get-tuple-element.11.rsd0.rsd1, f32[8,8192,128]{2,1,0:T(8,128)} %get-tuple-element.12.psm, f32[8,8192,128]{2,1,0:T(8,128)} %get-tuple-element.13.rsm, ...), custom_call_target="tpu_custom_call" | custom-call | tf_op jit(solution)/shard_map/assemble/pallas_call | solution.py:527

commit v3 on v2

v3 whole, which is shorter than its diff:
```python
import functools

import jax
import jax.numpy as jnp
from jax import lax
from jax.experimental import pallas as pl
from jax.experimental.pallas import tpu as pltpu
from jax.sharding import PartitionSpec as P

MESH = pl.DeviceIdType.MESH
LANE = 128

SPLIT = ((14, 2), (4, 1))

PLAN = (
    (
        "ISSISXSSIIIIIXXASSIISSIAXSSIAAXSSSSIAXSXSXISAASIXX",
        "XSSXIAAIISXAAXAAISXSXXAAXAAA",
    ),
    (
        "IXIIIIIIAXXFIXIXXAIIXAAXAXIXFFAFAIXAIIFAAIIFFXXFFA",
        "XFFAXFAFAIFXXAFAAXFFFA",
    ),
    (
        "IIIRRIIRXIIRAIXRXXIIRIAXIXRRFIIAAXIIXRRFFARAXIAFXR",
        "AAFAXRXFIAFFRAXXARXARFRAFXXFFAFARFXFFAFF",
    ),
    (
        "SISRSSSIISISSIXRSSXSSIRSISRASRRSASSXXIXAXIRISSARIA",
        "AXRIXRXAASIASSRXRXSXIRXARAXARIRARAXIXIAIXRXAAA",
    ),
)
STEPS = "IRXAFS"
WORD = 10


def plan_words():
    rows = []
    for pieces in PLAN:
        codes, count, kept = [], 0, False
        for step in "".join(pieces):
            codes.append(STEPS.index(step) + 1)
            if step == "S":
                codes[-1] += kept and count % 3 > 0
                count, kept = count + 1, True
            kept = kept and step != "X"
        rows.append([sum(code << (3 * k) for k, code in enumerate(codes[n:n + WORD])) for n in range(0, len(codes), WORD)])
    longest = max(len(row) for row in rows)
    return [row + [0] * (longest - len(row)) for row in rows]


class Sizes:
    def __init__(self, layers, rows, cols):
        self.layers, self.rows, self.cols = layers, rows, cols
        self.half = layers // 2
        self.tile = rows // 2
        self.units = rows // LANE
        self.sub = self.tile // LANE
        self.full = self.sub * self.tile
        self.pairs = (self.sub + 1) // 2
        self.low = self.sub * (self.sub - 1) // 2
        self.diag = (self.low + self.pairs) * LANE + (self.pairs + 7) // 8 * 8
        self.own = 2 * self.diag + self.full
        self.mid = 4 * self.full
        self.all_units = self.half * self.units
        self.chunks = sum(count for count, _ in SPLIT)
        self.depth = cols // 4 if cols % (4 * LANE) == 0 else cols


def triangles():
    row = lax.broadcasted_iota(jnp.int32, (LANE, LANE), 0)
    col = lax.broadcasted_iota(jnp.int32, (LANE, LANE), 1)
    return row >= col, row == col


def loop(lo, hi, f):
    def body(n, carry):
        f(n)
        return carry

    lax.fori_loop(lo, hi, body, 0)


def exchange_kernel(sz, a, r, lp, rp, psd, psm, rsd, rsm, pc, rb, co, v, acc, stage, cross_stage, ba, bb,
                    load_sem, xs, xr, ls, lr, ds, dr, ss, sr, rss, rsr, cs, cr, fs):
    y = lax.axis_index("kk")
    g = lax.axis_index("g")
    x = g // 2
    c = g % 2
    away = c == x
    home = c != x
    layers, half, units = sz.layers, sz.half, sz.units

    to_x = {"g": (g + 2) % 4}
    to_core = {"g": 2 * x + 1 - c}
    to_y = {"kk": 1 - y}

    def remote(src, dst, send, recv, where):
        return pltpu.make_async_remote_copy(src_ref=src, dst_ref=dst, send_sem=send, recv_sem=recv, device_id=where,
                                            device_id_type=MESH)

    def sized(f):
        def run(q):
            chunk, unit = 0, 0
            for count, size in SPLIT:
                @pl.when((q >= chunk) & (q < chunk + count))
                def _():
                    f(q, unit + (q - chunk) * size, size)

                chunk, unit = chunk + count, unit + count * size

        return run

    def rows_of(ref, u, size, first=0):
        return ref.at[first + u // units, pl.ds(pl.multiple_of(u % units * LANE, LANE), size * LANE)]

    def x_in(q, u, size):
        return remote(rows_of(a, u, size, half * (1 - x)), rows_of(r, u, size), xs.at[q], xr.at[q], to_x)

    def core_in(m):
        return remote(a.at[m], lp.at[m], ls.at[m], lr.at[m], to_core)

    def core_r(q, u, size):
        return remote(rows_of(r, u, size), rows_of(rp, u, size), ds.at[q], dr.at[q], to_core)

    def send_diag(k, m, rows=None):
        src, dst = psd.at[k, m], rsd.at[k, m]
        if rows is not None:
            src, dst = src.at[rows], dst.at[rows]
        return remote(src, dst, ss.at[k, m], sr.at[k, m], to_y)

    def send_mid(m, rows=None):
        src, dst = psm.at[m], rsm.at[m]
        if rows is not None:
            src, dst = src.at[rows], dst.at[rows]
        return remote(src, dst, ss.at[2, m], sr.at[2, m], to_y)

    def send_part(q, u, size):
        return remote(pc.at[pl.ds(u, size), 1 - y], rb.at[pl.ds(u, size)], rss.at[q], rsr.at[q], to_y)

    def send_sum(q, u, size):
        where = {"kk": jnp.where(home, 1 - y, y), "g": jnp.where(home, g, (g + 2) % 4)}
        part = co.at[x, pl.ds(u, size), y]
        return remote(part, part, cs.at[q], cr.at[jnp.where(home, 0, 1), q], where)

    def from_x(q, u, size):
        part = co.at[1 - x, pl.ds(u, size), y]
        return remote(part, part, fs.at[q], cr.at[1, q], to_x)

    def forward(q, u, size):
        part = co.at[1 - x, pl.ds(u, size), y]
        return remote(part, part, fs.at[q], cr.at[2, q], to_y)

    def load(src, dst, k):
        pltpu.make_async_copy(src, dst, load_sem.at[k]).start()

    def loaded(dst, k):
        pltpu.make_async_copy(dst, dst, load_sem.at[k]).wait()

    def store(src, dst):
        copy = pltpu.make_async_copy(src, dst, load_sem.at[4])
        copy.start()
        copy.wait()

    def block(n, rows=sz.rows):
        return v.at[pl.ds(pl.multiple_of(n, LANE), rows)]

    def product(left, right, width):
        acc[:, :width] = jnp.zeros((sz.tile, width), jnp.float32)

        def step(k):
            cols = pl.ds(pl.multiple_of(k * sz.depth, LANE), sz.depth)
            lhs = v[pl.ds(pl.multiple_of(left, LANE), sz.tile), cols]
            rhs = v[pl.ds(pl.multiple_of(right, LANE), width), cols]
            acc[:, :width] += lax.dot_general(lhs, rhs, (((1,), (1,)), ((), ())), preferred_element_type=jnp.float32)

        loop(0, sz.cols // sz.depth, step)

    def put_strips():
        for s in range(sz.sub):
            stage[s * sz.tile:(s + 1) * sz.tile, :] = acc[:, s * LANE:(s + 1) * LANE]

    def put_diag():
        def subtile(i, k):
            return acc[i * LANE:(i + 1) * LANE, k * LANE:(k + 1) * LANE]

        n = 0
        for i in range(sz.sub):
            for k in range(i):
                stage[n:n + LANE, :] = subtile(i, k)
                n += LANE
        lower, equal = triangles()
        tail = (sz.low + sz.pairs) * LANE
        stage[tail:sz.diag, :] = jnp.zeros((sz.diag - tail, LANE), jnp.float32)
        for i in range(0, sz.sub, 2):
            if i + 1 < sz.sub:
                other = subtile(i + 1, i + 1)
                stage[n:n + LANE, :] = jnp.where(lower, subtile(i, i), other)
                stage[tail + i // 2:tail + i // 2 + 1, :] = jnp.sum(jnp.where(equal, other, 0.0), axis=0, keepdims=True)
            else:
                stage[n:n + LANE, :] = subtile(i, i)
            n += LANE

    def same_chip(n, kept):
        m, k = n // 3, n % 3

        def halves(ref, at):
            for d in range(2):
                load(ref.at[m, pl.ds(d * sz.tile, sz.tile)], block(at + d * sz.tile, sz.tile), d)

        @pl.when(k == 0)
        def _():
            halves(a, 0)

        @pl.when((k == 2) & (kept == 0))
        def _():
            halves(lp, sz.rows)

        @pl.when(k == 1)
        def _():
            core_in(m).wait_recv()

            @pl.when(kept == 0)
            def _():
                load(a.at[m], block(0), 2)
                loaded(block(0), 2)

            load(lp.at[m], block(sz.rows), 3)
            loaded(block(sz.rows), 3)

            def middle(i):
                product(i // 2 * sz.tile + (1 - x) * sz.rows, i % 2 * sz.tile + x * sz.rows, sz.tile)
                put_strips()
                rows = pl.ds(pl.multiple_of(i * sz.full, LANE), sz.full)
                store(stage.at[pl.ds(0, sz.full)], psm.at[m, rows])
                send_mid(m, rows).start()

            loop(0, 4, middle)

        @pl.when(k != 1)
        def _():
            which = k // 2
            base = which * sz.rows

            def leave(lo, size):
                rows = pl.ds(pl.multiple_of(lo, 8), size)
                store(stage.at[pl.ds(0, size)], psd.at[which, m, rows])
                send_diag(which, m, rows).start()

            def diagonal(d):
                @pl.when((k == 0) | (kept == 0))
                def _():
                    loaded(block(base + d * sz.tile, sz.tile), d)

                product(base + d * sz.tile, base + d * sz.tile, sz.tile)
                put_diag()
                leave(d * sz.diag, sz.diag)

            loop(0, 2, diagonal)
            product(base + sz.tile, base, sz.tile)
            put_strips()
            leave(2 * sz.diag, sz.full)

    def relay(q, u, size):
        x_in(q, u, size).wait_recv()
        core_r(q, u, size).start()

    def cross(q, u, size):
        j, width = u // units, size * LANE

        @pl.when(x == 0)
        def _():
            @pl.when(home & (u % units == 0))
            def _():
                core_in(j).wait_recv()

            load(a.at[j], block(c * sz.rows), 0)
            load(lp.at[j], block((1 - c) * sz.rows), 1)
            x_in(q, u, size).wait_recv()
            load(rows_of(r, u, size), block(2 * sz.rows, width), 2)
            loaded(block(c * sz.rows), 0)
            loaded(block((1 - c) * sz.rows), 1)
            loaded(block(2 * sz.rows, width), 2)

            def one(n):
                product(n * sz.tile, 2 * sz.rows, width)
                for s in range(size):
                    rows = pl.ds(pl.multiple_of(n % 2 * sz.tile, LANE), sz.tile)
                    cross_stage[s, n // 2, rows, :] = acc[:, s * LANE:(s + 1) * LANE]

            loop(0, 4, one)

        @pl.when(x == 1)
        def _():
            load(a.at[half + j], block(2 * sz.rows), 0)
            load(rows_of(r, u, size), block(c * width, width), 1)
            core_r(q, u, size).wait_recv()
            load(rows_of(rp, u, size), block((1 - c) * width, width), 2)
            loaded(block(2 * sz.rows), 0)
            loaded(block(c * width, width), 1)
            loaded(block((1 - c) * width, width), 2)

            def one(t):
                product(2 * sz.rows + t * sz.tile, 0, 2 * width)
                for i in range(2):
                    for s in range(size):
                        rows = pl.ds(pl.multiple_of(t * sz.tile, LANE), sz.tile)
                        cross_stage[s, i, rows, :] = acc[:, i * width + s * LANE:i * width + (s + 1) * LANE]

            loop(0, 2, one)

        store(cross_stage.at[pl.ds(0, size)], pc.at[pl.ds(u, size)])
        send_part(q, u, size).start()

    def add(q, u, size):
        mine, theirs = ba.at[pl.ds(0, size)], bb.at[pl.ds(0, size)]
        load(pc.at[pl.ds(u, size), y], mine, 0)
        send_part(q, u, size).wait_recv()
        load(rb.at[pl.ds(u, size)], theirs, 1)
        loaded(mine, 0)
        loaded(theirs, 1)
        ba[:size] += bb[:size]
        store(mine, co.at[x, pl.ds(u, size), y])
        send_sum(q, u, size).start()

    def pass_on(q, u, size):
        from_x(q, u, size).wait_recv()
        forward(q, u, size).start()

    barrier = pltpu.get_barrier_semaphore()
    for where in (to_x, to_core, to_y):
        pl.semaphore_signal(barrier, inc=1, device_id=where, device_id_type=MESH)
    pl.semaphore_wait(barrier, 3)

    @pl.when(home)
    def _():
        loop(0, layers, lambda m: core_in(m).start())

    @pl.when(away & (x == 0))
    def _():
        loop(0, half, lambda m: core_in(m).start())

    steps = [sized(lambda *chunk: x_in(*chunk).start()), sized(relay), sized(cross), sized(add), sized(pass_on)]
    words = plan_words()

    def word(n, done):
        code = jnp.int32(0)
        for device, row in enumerate(words):
            for k, value in enumerate(row):
                code = jnp.where((g == device) & (n == k), value, code)

        def digit(_, carry):
            code, done = carry[0], list(carry[1:])
            now = code % 8
            for k, step in enumerate(steps):
                pl.when(now == k + 1)(functools.partial(step, done[k]))
                done[k] += jnp.where(now == k + 1, 1, 0)
            pl.when(now > len(steps))(functools.partial(same_chip, done[-1], now - len(steps) - 1))
            done[-1] += jnp.where(now > len(steps), 1, 0)
            return (code // 8, *done)

        return lax.fori_loop(0, WORD, digit, (code, *done))[1:]

    lax.fori_loop(0, len(words[0]), word, (jnp.int32(0),) * (len(steps) + 1))

    @pl.when(home)
    def _():
        loop(0, layers, lambda m: core_in(m).wait_send())

        def end(*chunk):
            send_sum(*chunk).wait_recv()
            forward(*chunk).wait_recv()
            forward(*chunk).wait_send()

        loop(0, sz.chunks, sized(end))

    @pl.when(away & (x == 0))
    def _():
        loop(0, half, lambda m: core_in(m).wait_send())

    @pl.when(x == 1)
    def _():
        loop(0, sz.chunks, sized(lambda *chunk: core_r(*chunk).wait_send()))

    @pl.when(away)
    def _():
        def end(m):
            for k in range(2):
                send_diag(k, m).wait()
            send_mid(m).wait()

        loop(0, layers, end)

    def sent(*chunk):
        x_in(*chunk).wait_send()
        send_part(*chunk).wait_send()
        send_sum(*chunk).wait_send()

    loop(0, sz.chunks, sized(sent))


def exchange(sz, a):
    f32, bf16 = jnp.float32, jnp.bfloat16
    dma = pltpu.SemaphoreType.DMA
    rows = (sz.rows, sz.cols)
    strip = (sz.rows, LANE)
    most = max(size for _, size in SPLIT)
    outs = [
        ((sz.half,) + rows, bf16),
        ((sz.layers,) + rows, bf16),
        ((sz.half,) + rows, bf16),
        ((2, sz.layers, sz.own, LANE), f32),
        ((sz.layers, sz.mid, LANE), f32),
        ((2, sz.layers, sz.own, LANE), f32),
        ((sz.layers, sz.mid, LANE), f32),
        ((sz.all_units, 2) + strip, f32),
        ((sz.all_units,) + strip, f32),
        ((2, sz.all_units, 2) + strip, f32),
    ]
    n, q = sz.layers, sz.chunks
    res = pl.pallas_call(
        functools.partial(exchange_kernel, sz),
        name="exchange",
        out_shape=[jax.ShapeDtypeStruct(s, d) for s, d in outs],
        in_specs=[pl.BlockSpec(memory_space=pl.ANY)],
        out_specs=[pl.BlockSpec(memory_space=pl.ANY)] * len(outs),
        scratch_shapes=[
            pltpu.VMEM((3 * sz.rows, sz.cols), bf16),
            pltpu.VMEM((sz.tile, sz.tile), f32),
            pltpu.VMEM((sz.full, LANE), f32),
            pltpu.VMEM((most, 2) + strip, f32),
            pltpu.VMEM((most,) + strip, f32),
            pltpu.VMEM((most,) + strip, f32),
            dma((5,)), dma((q,)), dma((q,)), dma((n,)), dma((n,)), dma((q,)), dma((q,)),
            dma((3, n)), dma((3, n)), dma((q,)), dma((q,)), dma((q,)), dma((3, q)), dma((q,)),
        ],
        compiler_params=pltpu.CompilerParams(collective_id=0, has_side_effects=True, vmem_limit_bytes=60 * 2**20),
    )(a)
    return res[3], res[5], res[4], res[6], res[9]


OUTS = 5
INS = 6
DIAGS = 4
ZERO_ROWS = 256


def assemble_kernel(sz, role, psd, rsd, psm, rsm, co, out, ob, ib, db, zeros, out_sem, in_sem, diag_sem, zero_sem):
    t, sub, layers, units = sz.tile, sz.sub, sz.layers, sz.units
    x = role[1]
    lower, equal = triangles()

    def copy(src, dst, sem):
        return pltpu.make_async_copy(src, dst, sem)

    def put(n, i, k, value):
        def at(s):
            return pl.ds(s * LANE if isinstance(s, int) else pl.multiple_of(s * LANE, LANE), LANE)

        ob[n % OUTS, at(i), at(k)] = value

    def free(n):
        @pl.when(n >= OUTS)
        def _():
            copy(ob.at[n % OUTS], out.at[0, 0], out_sem.at[n % OUTS]).wait()

    def leave(n, slot, m):
        copy(ob.at[n % OUTS], out.at[slot, m], out_sem.at[n % OUTS]).start()

    def drain():
        for n in range(OUTS):
            copy(ob.at[n], out.at[0, 0], out_sem.at[n]).wait()

    @pl.when(role[0] == 0)
    def _():
        zeros[...] = jnp.zeros_like(zeros)
        per = sz.rows // ZERO_ROWS

        def zero(n):
            rows = pl.ds(pl.multiple_of(n % per * ZERO_ROWS, ZERO_ROWS), ZERO_ROWS)
            return copy(zeros, out.at[2, n // per, rows], zero_sem)

        def fetch(n):
            m, slot = n // 2, n % 2
            first = m % sz.half * units
            return copy(co.at[m // sz.half, pl.ds(first, units), slot], ib.at[n % INS], in_sem.at[n % INS])

        loop(0, INS, lambda n: fetch(n).start())
        loop(0, layers * per, lambda n: zero(n).start())

        def one(n):
            m, slot = n // 2, n % 2
            fetch(n).wait()
            free(n)

            def unit(u):
                def strip(k):
                    return ib[n % INS, u, k * LANE:(k + 1) * LANE, :]

                @pl.when(m < sz.half)
                def _():
                    for k in range(2 * sub):
                        put(n, u, k, strip(k).T)

                @pl.when(m >= sz.half)
                def _():
                    for k in range(2 * sub):
                        put(n, k, u, strip(k))

            loop(0, units, unit)
            leave(n, slot, m)

            @pl.when(n + INS < 2 * layers)
            def _():
                fetch(n + INS).start()

        loop(0, 2 * layers, one)
        drain()
        loop(0, layers * per, lambda n: zero(n).wait())

    @pl.when(role[0] == 1)
    def _():
        def fetch_diag(n, go):
            for ref, k in ((psd, 0), (rsd, 1)):
                slot = 2 * (n % (DIAGS // 2)) + k
                go(copy(ref.at[n % 2, n // 2], db.at[slot], diag_sem.at[slot]))

        def fetch_mid(m, go):
            for ref, k in ((psm, 0), (rsm, 1)):
                slot = 2 * (m % (INS // 2)) + k
                go(copy(ref.at[m], ib.at[slot], in_sem.at[slot]))

        def start(c):
            c.start()

        def wait(c):
            c.wait()

        def diagonal(n, d):
            fetch_diag(d, wait)
            free(n)
            mine = 2 * (d % (DIAGS // 2))

            def total(row, size=LANE):
                return db[mine, row:row + size, :] + db[mine + 1, row:row + size, :]

            for e in range(2):
                row, first = e * sz.diag, e * sub
                tail = row + (sz.low + sz.pairs) * LANE
                for i in range(sub):
                    for k in range(i):
                        s = total(row)
                        put(n, first + i, first + k, s)
                        put(n, first + k, first + i, s.T)
                        row += LANE
                for i in range(0, sub, 2):
                    s = total(row)
                    flip = s.T
                    put(n, first + i, first + i, jnp.where(lower, s, flip))
                    if i + 1 < sub:
                        line = jnp.broadcast_to(total(tail + i // 2, 1), (LANE, LANE))
                        put(n, first + i + 1, first + i + 1, jnp.where(equal, line, jnp.where(lower, flip, s)))
                    row += LANE
            for k in range(sub):
                for i in range(sub):
                    s = total(2 * sz.diag + k * t + i * LANE)
                    put(n, sub + i, k, s)
                    put(n, k, sub + i, s.T)

        def middle(n, m):
            fetch_mid(m, wait)
            free(n)
            mine = 2 * (m % (INS // 2))

            def strips(u):
                tile, col = u // sub, u % sub
                for i in range(sub):
                    rows = pl.ds(pl.multiple_of(u % 2 * t + i * LANE, LANE), LANE)
                    s = ib[mine, u // 2, rows, :] + ib[mine + 1, u // 2, rows, :]
                    put(n, tile // 2 * sub + i, tile % 2 * sub + col, s)

            loop(0, 4 * sub, strips)

        loop(0, DIAGS // 2, lambda d: fetch_diag(d, start))
        loop(0, INS // 2, lambda m: fetch_mid(m, start))

        def one(m):
            def side(k):
                d = 2 * m + k
                n = 3 * m + k
                diagonal(n, d)
                leave(n, 2 * (x + k - 2 * x * k), m)

                @pl.when(d + DIAGS // 2 < 2 * layers)
                def _():
                    fetch_diag(d + DIAGS // 2, start)

            loop(0, 2, side)
            n = 3 * m + 2
            middle(n, m)
            leave(n, 1, m)

            @pl.when(m + INS // 2 < layers)
            def _():
                fetch_mid(m + INS // 2, start)

        loop(0, layers, one)
        drain()


def assemble(sz, role, psd, rsd, psm, rsm, co):
    f32, dma = jnp.float32, pltpu.SemaphoreType.DMA
    block = (sz.units, sz.rows, LANE)
    hbm = pl.BlockSpec(memory_space=pl.ANY)
    return pl.pallas_call(
        functools.partial(assemble_kernel, sz),
        name="assemble",
        out_shape=jax.ShapeDtypeStruct((3, sz.layers, sz.rows, sz.rows), f32),
        in_specs=[pl.BlockSpec(memory_space=pltpu.SMEM)] + [hbm] * 5,
        out_specs=hbm,
        scratch_shapes=[
            pltpu.VMEM((OUTS, sz.rows, sz.rows), f32),
            pltpu.VMEM((INS,) + block, f32),
            pltpu.VMEM((DIAGS, sz.own, LANE), f32),
            pltpu.VMEM((ZERO_ROWS, sz.rows), f32),
            dma((OUTS,)), dma((INS,)), dma((DIAGS,)), dma,
        ],
        compiler_params=pltpu.CompilerParams(vmem_limit_bytes=60 * 2**20),
    )(role, psd, rsd, psm.reshape((-1,) + block), rsm.reshape((-1,) + block), co)


def solution(mesh):
    def local_part(a_loc):
        sz = Sizes(*a_loc.shape)
        g = lax.axis_index("g")
        x, c = g // 2, g % 2
        role = jnp.stack([jnp.where(c == x, 1, 0), x]).astype(jnp.int32)
        return assemble(sz, role, *exchange(sz, a_loc))[None]

    return jax.shard_map(local_part, mesh=mesh, in_specs=(P(None, ("m", "g"), "kk"),), out_specs=P(("m", "g"), None, None, None, None), check_vma=False)
```

time: 1560 us -> 1540 us (0.987)
  Pallas kernels: 1560 us -> 1540 us
where the time goes in v3:
time: 1540 us
  Pallas kernels  1540 us (100%)
    pallas_call x1, Pallas kernels, exchange(): pl.pallas_call(functools.partial(exchange_kernel, sz), name='exchange', o...  1480 us
    pallas_call x1, Pallas kernels, assemble(): pl.pallas_call(functools.partial(assemble_kernel, sz), name='assemble', o...  55.5 us

profile of v3, /device:TPU:1, one launch (start us, length us, event | category | flops | bytes accessed | tf_op | source)
XLA Modules:
  0.0 1539.2 jit_solution(9074215333935834892)
XLA Ops:
  0.0 0.6 pad_add_fusion.role
  0.6 1483.1 %exchange.1 = (bf16[4,1024,7168]{2,1,0:T(8,128)(2,1)}, bf16[8,1024,7168]{2,1,0:T(8,128)(2,1)}, bf16[4,1024,7168]{2,1,0:T(8,128)(2,1)}, f32[2,8,4112,128]{3,2,1,0...) custom-call(bf16[8,1024,7168]{2,1,0:T(8,128)(2,1)} %a.1), custom_call_target="tpu_custom_call" | custom-call | tf_op jit(solution)/shard_map/exchange/pallas_call | solution.py:421
  1483.7 55.5 %assemble.1 = f32[3,8,1024,1024]{3,2,1,0:T(8,128)} custom-call(s32[2]{0:T(128)} %pad_add_fusion.role, f32[2,8,4112,128]{3,2,1,0:T(8,128)} %get-tuple-element.10.psd, f32[2,8,4112,128]{3,2,1,0:T(8,128)} %get-tuple-element.11.rsd, f32[8,8,1024,128]{3,2,1,0:T(8,128)} %bitcast.5, f32[8,8,1024,128]{3,2,1,0:T(8,128)} %bitcast.6, ...), custom_call_target="tpu_custom_call" | custom-call | tf_op jit(solution)/shard_map/assemble/pallas_call | solution.py:615

commit v4 on v3

--- a/solution.py
+++ b/solution.py
@@ -7,6 +7,7 @@
 from jax.experimental.pallas import tpu as pltpu
 from jax.sharding import PartitionSpec as P
 
+
 MESH = pl.DeviceIdType.MESH
 LANE = 128
 
@@ -14,20 +15,20 @@
 
 PLAN = (
     (
-        "ISSISXSSIIIIIXXASSIISSIAXSSIAAXSSSSIAXSXSXISAASIXX",
-        "XSSXIAAIISXAAXAAISXSXXAAXAAA",
+        "IIISSISSXIISXASSIIIIIIIIIIIIXASXASSXASXASSXASXSSXA",
+        "SXASASXASXASXSASAXXXXSXAAAAA",
     ),
     (
-        "IXIIIIIIAXXFIXIXXAIIXAAXAXIXFFAFAIXAIIFAAIIFFXXFFA",
-        "XFFAXFAFAIFXXAFAAXFFFA",
+        "IIIIXAIXAIXAIXAIXAIIXXAAIXAIXFFAFIXIFAIXFIFAIIXFAX",
+        "FAXFFAXXFAAXFAXFA",
     ),
     (
-        "IIIRRIIRXIIRAIXRXXIIRIAXIXRRFIIAAXIIXRRFFARAXIAFXR",
-        "AAFAXRXFIAFFRAXXARXARFRAFXXFFAFARFXFFAFF",
+        "IIIIIIRXIARXARXIARXIARXFIARXIRARXIAXIARXIARXIAIRXI",
+        "AIRXARXARXRXAARXARXARFXFFAFFFFFFFFF",
     ),
     (
-        "SISRSSSIISISSIXRSSXSSIRSISRASRRSASSXXIXAXIRISSARIA",
-        "AXRIXRXAASIASSRXRXSXIRXARAXARIRARAXIXIAIXRXAAA",
+        "ISSRIIIIISSISRSIXXRSSIXAARSSXARSIXARSXISARSAXRISXS",
+        "RASIAXRSSIXRASXARSISXIRASIXARSIXRXRAAAXRAXRAXA",
     ),
 )
 STEPS = "IRXAFS"
@@ -47,6 +48,9 @@
         rows.append([sum(code << (3 * k) for k, code in enumerate(codes[n:n + WORD])) for n in range(0, len(codes), WORD)])
     longest = max(len(row) for row in rows)
     return [row + [0] * (longest - len(row)) for row in rows]
+
+
+LATE = 3
 
 
 class Sizes:
@@ -64,6 +68,9 @@
         self.mid = 4 * self.full
         self.all_units = self.half * self.units
         self.chunks = sum(count for count, _ in SPLIT)
+        self.late = LATE
+        self.lead = self.units - 2 * LATE
+        self.early_units = self.all_units - 2 * LATE
         self.depth = cols // 4 if cols % (4 * LANE) == 0 else cols
 
 
@@ -81,7 +88,7 @@
     lax.fori_loop(lo, hi, body, 0)
 
 
-def exchange_kernel(sz, a, r, lp, rp, psd, psm, rsd, rsm, pc, rb, co, v, acc, stage, cross_stage, ba, bb,
+def exchange_kernel(sz, a, r, lp, rp, psd, psm, rsd, rsm, pc, rb, co, late_diag, late_lo, late_hi, v, acc, stage, cross_stage, ba, bb,
                     load_sem, xs, xr, ls, lr, ds, dr, ss, sr, rss, rsr, cs, cr, fs):
     y = lax.axis_index("kk")
     g = lax.axis_index("g")
@@ -244,8 +251,15 @@
 
             def leave(lo, size):
                 rows = pl.ds(pl.multiple_of(lo, 8), size)
-                store(stage.at[pl.ds(0, size)], psd.at[which, m, rows])
-                send_diag(which, m, rows).start()
+
+                @pl.when(n == 3 * layers - 1)
+                def _():
+                    store(stage.at[pl.ds(0, size)], late_diag.at[rows])
+
+                @pl.when(n < 3 * layers - 1)
+                def _():
+                    store(stage.at[pl.ds(0, size)], psd.at[which, m, rows])
+                    send_diag(which, m, rows).start()
 
             def diagonal(d):
                 @pl.when((k == 0) | (kept == 0))
@@ -320,8 +334,20 @@
         loaded(mine, 0)
         loaded(theirs, 1)
         ba[:size] += bb[:size]
-        store(mine, co.at[x, pl.ds(u, size), y])
-        send_sum(q, u, size).start()
+        over = u - sz.early_units
+
+        @pl.when(home | (over < 0))
+        def _():
+            store(mine, co.at[x, pl.ds(u, size), y])
+            send_sum(q, u, size).start()
+
+        @pl.when(away & (over >= 0) & (over < sz.late))
+        def _():
+            store(mine, late_lo.at[pl.ds(over, size)])
+
+        @pl.when(away & (over >= sz.late))
+        def _():
+            store(mine, late_hi.at[pl.ds(over - sz.late, size)])
 
     def pass_on(q, u, size):
         from_x(q, u, size).wait_recv()
@@ -367,10 +393,13 @@
     def _():
         loop(0, layers, lambda m: core_in(m).wait_send())
 
-        def end(*chunk):
-            send_sum(*chunk).wait_recv()
-            forward(*chunk).wait_recv()
-            forward(*chunk).wait_send()
+        def end(q, u, size):
+            send_sum(q, u, size).wait_recv()
+
+            @pl.when(u < sz.early_units)
+            def _():
+                forward(q, u, size).wait_recv()
+                forward(q, u, size).wait_send()
 
         loop(0, sz.chunks, sized(end))
 
@@ -385,16 +414,22 @@
     @pl.when(away)
     def _():
         def end(m):
-            for k in range(2):
-                send_diag(k, m).wait()
+            send_diag(0, m).wait()
             send_mid(m).wait()
 
+            @pl.when(m < layers - 1)
+            def _():
+                send_diag(1, m).wait()
+
         loop(0, layers, end)
 
-    def sent(*chunk):
-        x_in(*chunk).wait_send()
-        send_part(*chunk).wait_send()
-        send_sum(*chunk).wait_send()
+    def sent(q, u, size):
+        x_in(q, u, size).wait_send()
+        send_part(q, u, size).wait_send()
+
+        @pl.when(home | (u < sz.early_units))
+        def _():
+            send_sum(q, u, size).wait_send()
 
     loop(0, sz.chunks, sized(sent))
 
@@ -416,6 +451,9 @@
         ((sz.all_units, 2) + strip, f32),
         ((sz.all_units,) + strip, f32),
         ((2, sz.all_units, 2) + strip, f32),
+        ((sz.own, LANE), f32),
+        ((sz.late,) + strip, f32),
+        ((sz.late,) + strip, f32),
     ]
     n, q = sz.layers, sz.chunks
     res = pl.pallas_call(
@@ -436,99 +474,162 @@
         ],
         compiler_params=pltpu.CompilerParams(collective_id=0, has_side_effects=True, vmem_limit_bytes=60 * 2**20),
     )(a)
-    return res[3], res[5], res[4], res[6], res[9]
+    return (res[3], res[5], res[4], res[6], res[9]), res[10:]
 
 
 OUTS = 5
 INS = 6
 DIAGS = 4
 ZERO_ROWS = 256
-
-
-def assemble_kernel(sz, role, psd, rsd, psm, rsm, co, out, ob, ib, db, zeros, out_sem, in_sem, diag_sem, zero_sem):
-    t, sub, layers, units = sz.tile, sz.sub, sz.layers, sz.units
+HOME_PARTS = (0, 4, 9, 14)
+AWAY_PARTS = (0, 3, 6, 8)
+
+
+class Blocks:
+    def __init__(self, sz, out, ob, out_sem):
+        self.sz, self.out, self.ob, self.out_sem = sz, out, ob, out_sem
+        self.lower, self.equal = triangles()
+
+    def put(self, b, i, k, value):
+        def at(n):
+            return pl.ds(n * LANE if isinstance(n, int) else pl.multiple_of(n * LANE, LANE), LANE)
+
+        self.ob[b, at(i), at(k)] = value
+
+    def free(self, n):
+        @pl.when(n >= OUTS)
+        def _():
+            self.done(n % OUTS)
+
+    def leave(self, n, slot, m):
+        b = n % OUTS
+        pltpu.make_async_copy(self.ob.at[b], self.out.at[slot, m], self.out_sem.at[b]).start()
+
+    def done(self, b):
+        pltpu.make_async_copy(self.ob.at[b], self.out.at[0, 0], self.out_sem.at[b]).wait()
+
+    def drain(self, count):
+        for b in range(min(OUTS, count)):
+            self.done(b)
+
+    def unit(self, b, u, strip, transposed):
+        count = 2 * self.sz.sub
+
+        @pl.when(transposed)
+        def _():
+            for k in range(count):
+                self.put(b, u, k, strip(k).T)
+
+        @pl.when(jnp.logical_not(transposed))
+        def _():
+            for k in range(count):
+                self.put(b, k, u, strip(k))
+
+    def diagonal(self, b, total):
+        sz, sub = self.sz, self.sz.sub
+        for e in range(2):
+            row, first = e * sz.diag, e * sub
+            tail = row + (sz.low + sz.pairs) * LANE
+            for i in range(sub):
+                for k in range(i):
+                    s = total(row, LANE)
+                    self.put(b, first + i, first + k, s)
+                    self.put(b, first + k, first + i, s.T)
+                    row += LANE
+            for i in range(0, sub, 2):
+                s = total(row, LANE)
+                flip = s.T
+                self.put(b, first + i, first + i, jnp.where(self.lower, s, flip))
+                if i + 1 < sub:
+                    line = jnp.broadcast_to(total(tail + i // 2, 1), (LANE, LANE))
+                    other = jnp.where(self.equal, line, jnp.where(self.lower, flip, s))
+                    self.put(b, first + i + 1, first + i + 1, other)
+                row += LANE
+        for k in range(sub):
+            for i in range(sub):
+                s = total(2 * sz.diag + k * sz.tile + i * LANE, LANE)
+                self.put(b, sub + i, k, s)
+                self.put(b, k, sub + i, s.T)
+
+
+def assemble_kernel(sz, number, *refs):
+    first, late_mine, late_theirs = number == 0, None, None
+    role, psd, rsd, psm, rsm, co = refs[:6]
+    if AWAY_PARTS[number + 1] == sz.layers:
+        late_mine, late_theirs = refs[6:8]
+    out = refs[-9]
+    ob, ib, db, zeros, out_sem, in_sem, diag_sem, zero_sem = refs[-8:]
+    layers, half, units, sub, t = sz.layers, sz.half, sz.units, sz.sub, sz.tile
     x = role[1]
-    lower, equal = triangles()
-
-    def copy(src, dst, sem):
-        return pltpu.make_async_copy(src, dst, sem)
-
-    def put(n, i, k, value):
-        def at(s):
-            return pl.ds(s * LANE if isinstance(s, int) else pl.multiple_of(s * LANE, LANE), LANE)
-
-        ob[n % OUTS, at(i), at(k)] = value
-
-    def free(n):
-        @pl.when(n >= OUTS)
-        def _():
-            copy(ob.at[n % OUTS], out.at[0, 0], out_sem.at[n % OUTS]).wait()
-
-    def leave(n, slot, m):
-        copy(ob.at[n % OUTS], out.at[slot, m], out_sem.at[n % OUTS]).start()
-
-    def drain():
-        for n in range(OUTS):
-            copy(ob.at[n], out.at[0, 0], out_sem.at[n]).wait()
+    blocks = Blocks(sz, out, ob, out_sem)
 
     @pl.when(role[0] == 0)
     def _():
-        zeros[...] = jnp.zeros_like(zeros)
+        lo, hi = HOME_PARTS[number:number + 2]
         per = sz.rows // ZERO_ROWS
 
         def zero(n):
             rows = pl.ds(pl.multiple_of(n % per * ZERO_ROWS, ZERO_ROWS), ZERO_ROWS)
-            return copy(zeros, out.at[2, n // per, rows], zero_sem)
+            return pltpu.make_async_copy(zeros, out.at[2, n // per, rows], zero_sem)
+
+        def place(n):
+            over = jnp.where(n >= layers, 1, 0)
+            return x + over - 2 * x * over, n // 2 - over * half, n % 2
 
         def fetch(n):
-            m, slot = n // 2, n % 2
-            first = m % sz.half * units
-            return copy(co.at[m // sz.half, pl.ds(first, units), slot], ib.at[n % INS], in_sem.at[n % INS])
-
-        loop(0, INS, lambda n: fetch(n).start())
-        loop(0, layers * per, lambda n: zero(n).start())
+            side, j, slot = place(n)
+            b = (n - lo) % INS
+            return pltpu.make_async_copy(co.at[side, pl.ds(j * units, units), slot], ib.at[b], in_sem.at[b])
+
+        loop(lo, min(lo + INS, hi), lambda n: fetch(n).start())
+        if first:
+            zeros[...] = jnp.zeros_like(zeros)
+            loop(0, layers * per, lambda n: zero(n).start())
 
         def one(n):
-            m, slot = n // 2, n % 2
+            side, j, slot = place(n)
+            k = n - lo
             fetch(n).wait()
-            free(n)
+            blocks.free(k)
 
             def unit(u):
-                def strip(k):
-                    return ib[n % INS, u, k * LANE:(k + 1) * LANE, :]
-
-                @pl.when(m < sz.half)
-                def _():
-                    for k in range(2 * sub):
-                        put(n, u, k, strip(k).T)
-
-                @pl.when(m >= sz.half)
-                def _():
-                    for k in range(2 * sub):
-                        put(n, k, u, strip(k))
+                blocks.unit(k % OUTS, u, lambda i: ib[k % INS, u, i * LANE:(i + 1) * LANE, :], side == 0)
 
             loop(0, units, unit)
-            leave(n, slot, m)
-
-            @pl.when(n + INS < 2 * layers)
+            blocks.leave(k, slot, side * half + j)
+
+            @pl.when(n + INS < hi)
             def _():
                 fetch(n + INS).start()
 
-        loop(0, 2 * layers, one)
-        drain()
-        loop(0, layers * per, lambda n: zero(n).wait())
+        loop(lo, hi, one)
+        blocks.drain(hi - lo)
+        if first:
+            loop(0, layers * per, lambda n: zero(n).wait())
 
     @pl.when(role[0] == 1)
     def _():
-        def fetch_diag(n, go):
-            for ref, k in ((psd, 0), (rsd, 1)):
-                slot = 2 * (n % (DIAGS // 2)) + k
-                go(copy(ref.at[n % 2, n // 2], db.at[slot], diag_sem.at[slot]))
+        lo, hi = AWAY_PARTS[number:number + 2]
+        depth, diag_depth = INS // 2, DIAGS // 2
+
+        def fetch_diag(d, go):
+            for ref, late, k in ((psd, late_mine, 0), (rsd, late_theirs, 1)):
+                b = 2 * ((d - 2 * lo) % diag_depth) + k
+                if late is None:
+                    go(pltpu.make_async_copy(ref.at[d % 2, d // 2], db.at[b], diag_sem.at[b]))
+                else:
+                    @pl.when(d == 2 * layers - 1)
+                    def _():
+                        go(pltpu.make_async_copy(late, db.at[b], diag_sem.at[b]))
+
+                    @pl.when(d < 2 * layers - 1)
+                    def _():
+                        go(pltpu.make_async_copy(ref.at[d % 2, d // 2], db.at[b], diag_sem.at[b]))
 
         def fetch_mid(m, go):
             for ref, k in ((psm, 0), (rsm, 1)):
-                slot = 2 * (m % (INS // 2)) + k
-                go(copy(ref.at[m], ib.at[slot], in_sem.at[slot]))
+                b = 2 * ((m - lo) % depth) + k
+                go(pltpu.make_async_copy(ref.at[m], ib.at[b], in_sem.at[b]))
 
         def start(c):
             c.start()
@@ -536,87 +637,59 @@
         def wait(c):
             c.wait()
 
-        def diagonal(n, d):
-            fetch_diag(d, wait)
-            free(n)
-            mine = 2 * (d % (DIAGS // 2))
-
-            def total(row, size=LANE):
-                return db[mine, row:row + size, :] + db[mine + 1, row:row + size, :]
-
-            for e in range(2):
-                row, first = e * sz.diag, e * sub
-                tail = row + (sz.low + sz.pairs) * LANE
-                for i in range(sub):
-                    for k in range(i):
-                        s = total(row)
-                        put(n, first + i, first + k, s)
-                        put(n, first + k, first + i, s.T)
-                        row += LANE
-                for i in range(0, sub, 2):
-                    s = total(row)
-                    flip = s.T
-                    put(n, first + i, first + i, jnp.where(lower, s, flip))
-                    if i + 1 < sub:
-                        line = jnp.broadcast_to(total(tail + i // 2, 1), (LANE, LANE))
-                        put(n, first + i + 1, first + i + 1, jnp.where(equal, line, jnp.where(lower, flip, s)))
-                    row += LANE
-            for k in range(sub):
-                for i in range(sub):
-                    s = total(2 * sz.diag + k * t + i * LANE)
-                    put(n, sub + i, k, s)
-                    put(n, k, sub + i, s.T)
-
-        def middle(n, m):
+        loop(2 * lo, 2 * lo + diag_depth, lambda d: fetch_diag(d, start))
+        loop(lo, min(lo + depth, hi), lambda m: fetch_mid(m, start))
+
+        def one(m):
+            def side(k):
+                d, n = 2 * m + k, 3 * (m - lo) + k
+                mine = 2 * ((d - 2 * lo) % diag_depth)
+                fetch_diag(d, wait)
+                blocks.free(n)
+                blocks.diagonal(n % OUTS, lambda row, size: db[mine, row:row + size, :] + db[mine + 1, row:row + size, :])
+                blocks.leave(n, 2 * (x + k - 2 * x * k), m)
+
+                @pl.when(d + diag_depth < 2 * hi)
+                def _():
+                    fetch_diag(d + diag_depth, start)
+
+            loop(0, 2, side)
+            n = 3 * (m - lo) + 2
+            mine = 2 * ((m - lo) % depth)
             fetch_mid(m, wait)
-            free(n)
-            mine = 2 * (m % (INS // 2))
+            blocks.free(n)
 
             def strips(u):
                 tile, col = u // sub, u % sub
                 for i in range(sub):
                     rows = pl.ds(pl.multiple_of(u % 2 * t + i * LANE, LANE), LANE)
                     s = ib[mine, u // 2, rows, :] + ib[mine + 1, u // 2, rows, :]
-                    put(n, tile // 2 * sub + i, tile % 2 * sub + col, s)
+                    blocks.put(n % OUTS, tile // 2 * sub + i, tile % 2 * sub + col, s)
 
             loop(0, 4 * sub, strips)
-
-        loop(0, DIAGS // 2, lambda d: fetch_diag(d, start))
-        loop(0, INS // 2, lambda m: fetch_mid(m, start))
-
-        def one(m):
-            def side(k):
-                d = 2 * m + k
-                n = 3 * m + k
-                diagonal(n, d)
-                leave(n, 2 * (x + k - 2 * x * k), m)
-
-                @pl.when(d + DIAGS // 2 < 2 * layers)
-                def _():
-                    fetch_diag(d + DIAGS // 2, start)
-
-            loop(0, 2, side)
-            n = 3 * m + 2
-            middle(n, m)
-            leave(n, 1, m)
-
-            @pl.when(m + INS // 2 < layers)
+            blocks.leave(n, 1, m)
+
+            @pl.when(m + depth < hi)
             def _():
-                fetch_mid(m + INS // 2, start)
-
-        loop(0, layers, one)
-        drain()
-
-
-def assemble(sz, role, psd, rsd, psm, rsm, co):
+                fetch_mid(m + depth, start)
+
+        loop(lo, hi, one)
+        blocks.drain(3 * (hi - lo))
+
+
+def assemble(sz, number, role, parts, late=(), out=None):
     f32, dma = jnp.float32, pltpu.SemaphoreType.DMA
     block = (sz.units, sz.rows, LANE)
     hbm = pl.BlockSpec(memory_space=pl.ANY)
+    psd, rsd, psm, rsm, co = parts
+    args = [role, psd, rsd, psm.reshape((-1,) + block), rsm.reshape((-1,) + block), co, *late]
+    if out is not None:
+        args.append(out)
+    moved = sz.layers * sz.rows * sz.rows * 4 * 2
     return pl.pallas_call(
-        functools.partial(assemble_kernel, sz),
-        name="assemble",
+        functools.partial(assemble_kernel, sz, number),
         out_shape=jax.ShapeDtypeStruct((3, sz.layers, sz.rows, sz.rows), f32),
-        in_specs=[pl.BlockSpec(memory_space=pltpu.SMEM)] + [hbm] * 5,
+        in_specs=[pl.BlockSpec(memory_space=pltpu.SMEM)] + [hbm] * (len(args) - 1),
         out_specs=hbm,
         scratch_shapes=[
             pltpu.VMEM((OUTS, sz.rows, sz.rows), f32),
@@ -625,16 +698,125 @@
             pltpu.VMEM((ZERO_ROWS, sz.rows), f32),
             dma((OUTS,)), dma((INS,)), dma((DIAGS,)), dma,
         ],
+        input_output_aliases={} if out is None else {len(args) - 1: 0},
+        cost_estimate=pl.CostEstimate(flops=10**10, bytes_accessed=moved, transcendentals=0),
         compiler_params=pltpu.CompilerParams(vmem_limit_bytes=60 * 2**20),
-    )(role, psd, rsd, psm.reshape((-1,) + block), rsm.reshape((-1,) + block), co)
+    )(*args)
+
+
+def finish_kernel(sz, last, role, *refs):
+    count = 1 if last else 3
+    pieces, co, out = refs[:count], refs[count], refs[count + 2]
+    ob, ib, hb, out_sem, in_sem, head_sem = refs[-6:]
+    side = 1 - role[1]
+    m = side * sz.half + sz.half - 1
+    slots = role[2], 1 - role[2]
+    tail = sz.lead + sz.late
+    blocks = Blocks(sz, out, ob, out_sem)
+
+    @pl.when(role[0] == 0)
+    def _():
+        def heads(b):
+            first = (sz.half - 1) * sz.units
+            return pltpu.make_async_copy(co.at[side, pl.ds(first, sz.lead), slots[b]], hb.at[b], head_sem.at[b])
+
+        copies = [pltpu.make_async_copy(ref, ib.at[n], in_sem.at[n]) for n, ref in enumerate(pieces)]
+        for c in copies:
+            c.start()
+
+        def head(b):
+            heads(b).wait()
+            loop(0, sz.lead, lambda u: blocks.unit(b, u, lambda k: hb[b, u, k * LANE:(k + 1) * LANE, :], side == 0))
+
+        def units(n, b, first):
+            copies[n].wait()
+            loop(0, sz.late, lambda u: blocks.unit(b, first + u, lambda k: ib[n, u, k * LANE:(k + 1) * LANE, :], side == 0))
+
+        def part(b, first, size, go):
+            rows = pl.ds(first * LANE, size * LANE)
+
+            @pl.when(side == 0)
+            def _():
+                go(pltpu.make_async_copy(ob.at[b, rows], out.at[slots[b], m, rows], out_sem.at[b]))
+
+            @pl.when(side == 1)
+            def _():
+                go(pltpu.make_async_copy(ob.at[b, :, rows], out.at[slots[b], m, :, rows], out_sem.at[b]))
+
+        def start(c):
+            c.start()
+
+        def wait(c):
+            c.wait()
+
+        if last:
+            units(0, 1, tail)
+            part(1, tail, sz.late, start)
+            part(1, tail, sz.late, wait)
+        else:
+            heads(0).start()
+            heads(1).start()
+            head(0)
+            units(0, 0, sz.lead)
+            units(1, 0, tail)
+            blocks.leave(0, slots[0], m)
+            head(1)
+            units(2, 1, sz.lead)
+            part(1, 0, tail, start)
+            blocks.done(0)
+            part(1, 0, tail, wait)
+
+
+def finish(sz, last, role, pieces, co, out):
+    f32, dma = jnp.float32, pltpu.SemaphoreType.DMA
+    count = len(pieces)
+    hbm = pl.BlockSpec(memory_space=pl.ANY)
+    return pl.pallas_call(
+        functools.partial(finish_kernel, sz, last),
+        name="finish_last" if last else "finish",
+        out_shape=jax.ShapeDtypeStruct(out.shape, f32),
+        in_specs=[pl.BlockSpec(memory_space=pltpu.SMEM)] + [hbm] * (count + 2),
+        out_specs=hbm,
+        scratch_shapes=[
+            pltpu.VMEM((2, sz.rows, sz.rows), f32),
+            pltpu.VMEM((count, sz.late, sz.rows, LANE), f32),
+            pltpu.VMEM((2, sz.lead, sz.rows, LANE), f32),
+            dma((2,)), dma((count,)), dma((2,)),
+        ],
+        input_output_aliases={count + 2: 0},
+        cost_estimate=pl.CostEstimate(flops=3 * 10**9, bytes_accessed=8 * sz.rows * sz.rows, transcendentals=0),
+        compiler_params=pltpu.CompilerParams(vmem_limit_bytes=32 * 2**20),
+    )(role, *pieces, co, out)
 
 
 def solution(mesh):
+    width = mesh.shape["g"]
+    axes = ("kk", "g")
+
+    def pairs(moves):
+        return [(a * width + b, c * width + d) for (a, b), (c, d) in moves]
+
+    ys = range(mesh.shape["kk"])
+    over_x = pairs([((y, g), (y, (g + 2) % 4)) for y in ys for g in (0, 3)])
+    away_y = pairs([((y, g), (1 - y, g)) for y in ys for g in (0, 3)])
+    home_y = pairs([((y, g), (1 - y, g)) for y in ys for g in (1, 2)])
+
     def local_part(a_loc):
         sz = Sizes(*a_loc.shape)
         g = lax.axis_index("g")
         x, c = g // 2, g % 2
-        role = jnp.stack([jnp.where(c == x, 1, 0), x]).astype(jnp.int32)
-        return assemble(sz, role, *exchange(sz, a_loc))[None]
+        role = jnp.stack([jnp.where(c == x, 1, 0), x, lax.axis_index("kk")]).astype(jnp.int32)
+        parts, (late_diag, late_lo, late_hi) = exchange(sz, a_loc)
+        lo = lax.ppermute(late_lo, axes, over_x)
+        hi = lax.ppermute(late_hi, axes, over_x)
+        theirs = lax.ppermute(late_diag, axes, away_y)
+        lo_too = lax.ppermute(lo, axes, home_y)
+        hi_too = lax.ppermute(hi, axes, home_y)
+        out = assemble(sz, 0, role, parts)
+        out = assemble(sz, 1, role, parts, (), out)
+        out = assemble(sz, 2, role, parts, (late_diag, theirs), out)
+        out = finish(sz, False, role, (lo, hi, lo_too), parts[-1], out)
+        out = finish(sz, True, role, (hi_too,), parts[-1], out)
+        return out[None]
 
     return jax.shard_map(local_part, mesh=mesh, in_specs=(P(None, ("m", "g"), "kk"),), out_specs=P(("m", "g"), None, None, None, None), check_vma=False)

time: 1540 us -> 1540 us (level); the launches traced: 1540 us -> 1520 us
  Pallas kernels: 1540 us -> 1500 us
    pallas_call x1, Pallas kernels: 1480 us -> 1440 us  [exchange(): pl.pallas_call(functools.partial(exchange_kernel, sz), name='exchange', o...]
    pallas_call x1 -> x5, Pallas kernels: 55.5 us -> 62.7 us  [the longest x3 53.1 us: assemble(): pl.pallas_call(functools.partial(assemble_kernel, sz, number), out_shape=...]
  transfers between devices with their start and end apart: 0 -> 5, of which waited for: 0 -> 1; matrix products, arithmetic and copies ran while one was open for 0% -> 0% of each run, Pallas kernels for 0% -> 4%
where the time goes in v4:
time: 1540 us; the launch traced here: 1520 us
  Pallas kernels  1500 us (97%)
    pallas_call x1, Pallas kernels, exchange(): pl.pallas_call(functools.partial(exchange_kernel, sz), name='exchange', o...  1440 us
    pallas_call x3, Pallas kernels, assemble(): pl.pallas_call(functools.partial(assemble_kernel, sz, number), out_shape=...  53.1 us
  transfers between devices with their start and end apart: 5, of which 1 were waited for; matrix products, arithmetic and copies ran while one was open for 0% of the time, Pallas kernels for 4%

profile of v4, /device:TPU:1, one launch (start us, length us, event | category | flops | bytes accessed | tf_op | source)
XLA Modules:
  0.0 1522.3 jit_solution(16085529584501362509)
XLA Ops:
  0.0 1440.4 %exchange.1 = (bf16[4,1024,7168]{2,1,0:T(8,128)(2,1)}, bf16[8,1024,7168]{2,1,0:T(8,128)(2,1)}, bf16[4,1024,7168]{2,1,0:T(8,128)(2,1)}, f32[2,8,4112,128]{3,2,1,0...) custom-call(bf16[8,1024,7168]{2,1,0:T(8,128)(2,1)} %a.1), custom_call_target="tpu_custom_call" | custom-call | tf_op jit(solution)/shard_map/exchange/pallas_call | solution.py:459
  1440.4 1.3 collective-permute-start
  1441.7 1.3 collective-permute-start.2
  1443.0 2.0 collective-permute-start.4
  1444.9 0.6 pad_add_fusion.refs_0_.role
  1445.5 22.1 %shard_map.17.refs_6_ = f32[3,8,1024,1024]{3,2,1,0:T(8,128)} custom-call(s32[3]{0:T(128)} %pad_add_fusion.refs_0_.role, f32[2,8,4112,128]{3,2,1,0:T(8,128)} %get-tuple-element.16.refs_1_, f32[2,8,4112,128]{3,2,1,0:T(8,128)} %get-tuple-element.17.refs_2_, f32[8,8,1024,128]{3,2,1,0:T(8,128)} %bitcast.6, f32[8,8,1024,128]{3,2,1,0:T(8,128)} %bitcast.9, ...), custom_call_target="tpu_custom_call" | custom-call | flops 10000000000 | bytes 67108864 | tf_op jit(solution)/shard_map/pallas_call | solution.py:689
  1467.7 0.0 collective-permute-done.refs_1_
  1467.7 2.7 collective-permute-start.1
  1470.4 8.6 collective-permute-done.2.refs_0_
  1479.0 2.7 collective-permute-start.3
  1481.7 15.7 %shard_map.18.refs_8_ = f32[3,8,1024,1024]{3,2,1,0:T(8,128)} custom-call(s32[3]{0:T(128)} %pad_add_fusion.refs_0_.role, f32[2,8,4112,128]{3,2,1,0:T(8,128)} %get-tuple-element.16.refs_1_, f32[2,8,4112,128]{3,2,1,0:T(8,128)} %get-tuple-element.17.refs_2_, f32[8,8,1024,128]{3,2,1,0:T(8,128)} %bitcast.7, ...), custom_call_target="tpu_custom_call", output_to_operand_aliasing={{}: (6, {})} | custom-call | flops 10000000000 | bytes 67108864 | tf_op jit(solution)/shard_map/pallas_call | solution.py:689
  1497.3 0.0 copy-start
  1497.3 0.0 collective-permute-done.4.refs_7_
  1497.4 15.3 %shard_map.19.refs_4_ = f32[3,8,1024,1024]{3,2,1,0:T(8,128)} custom-call(s32[3]{0:T(128)} %pad_add_fusion.refs_0_.role, f32[2,8,4112,128]{3,2,1,0:T(8,128)} %get-tuple-element.16.refs_1_, f32[2,8,4112,128]{3,2,1,0:T(8,128)} %get-tuple-element.17.refs_2_, f32[8,8,1024,128]{3,2,1,0:T(8,128)} %bitcast.8, ...), custom_call_target="tpu_custom_call", output_to_operand_aliasing={{}: (8, {})} | custom-call | flops 10000000000 | bytes 67108864 | tf_op jit(solution)/shard_map/pallas_call | solution.py:689
  1512.6 0.0 collective-permute-done.3.refs_2_
  1512.7 0.0 copy-done
  1512.7 6.2 finish.1.refs_2_
  1518.9 0.0 collective-permute-done.1.refs_0_
  1518.9 3.4 finish_last.1
Async XLA Ops:
  1440.4 27.3 %collective-permute-start = (f32[3,1024,128]{2,1,0:T(8,128)}, f32[3,1024,128]{2,1,0:T(8,128)}, u32[]{:S(2)}, u32[]{:S(2)}) collective-permute-start(f32[3,1024,128]{2,1,0:T(8,128)} %get-tuple-element.13), channel_id=1, source_target_pairs={{0,2},{3,1},{4,6},{7,5}} | collective-permute-start | bytes 4718600 | tf_op jit(solution)/shard_map/ppermute | solution.py:811
  1441.7 37.3 %collective-permute-start.2 = (f32[3,1024,128]{2,1,0:T(8,128)}, f32[3,1024,128]{2,1,0:T(8,128)}, u32[]{:S(2)}, u32[]{:S(2)}) collective-permute-start(f32[3,1024,128]{2,1,0:T(8,128)} %get-tuple-element.15), channel_id=1, source_target_pairs={{0,2},{3,1},{4,6},{7,5}} | collective-permute-start | bytes 4718600 | tf_op jit(solution)/shard_map/ppermute | solution.py:810
  1443.0 54.4 %collective-permute-start.4 = (f32[4112,128]{1,0:T(8,128)}, f32[4112,128]{1,0:T(8,128)}, u32[]{:S(2)}, u32[]{:S(2)}) collective-permute-start(f32[4112,128]{1,0:T(8,128)} %get-tuple-element.20.refs_6_), channel_id=1, source_target_pairs={{0,4},{3,7},{4,0},{7,3}} | collective-permute-start | bytes 6316040 | tf_op jit(solution)/shard_map/ppermute | solution.py:812
  1467.7 51.2 %collective-permute-start.1 = (f32[3,1024,128]{2,1,0:T(8,128)}, f32[3,1024,128]{2,1,0:T(8,128)}, u32[]{:S(2)}, u32[]{:S(2)}) collective-permute-start(f32[3,1024,128]{2,1,0:T(8,128)} %collective-permute-done.refs_1_), channel_id=1, source_target_pairs={{1,5},{2,6},{5,1},{6,2}} | collective-permute-start | bytes 4718600 | tf_op jit(solution)/shard_map/ppermute | solution.py:814
  1479.0 33.7 %collective-permute-start.3 = (f32[3,1024,128]{2,1,0:T(8,128)}, f32[3,1024,128]{2,1,0:T(8,128)}, u32[]{:S(2)}, u32[]{:S(2)}) collective-permute-start(f32[3,1024,128]{2,1,0:T(8,128)} %collective-permute-done.2.refs_0_), channel_id=1, source_target_pairs={{1,5},{2,6},{5,1},{6,2}} | collective-permute-start | bytes 4718600 | tf_op jit(solution)/shard_map/ppermute | solution.py:813
  1497.3 15.3 %copy-start = (s32[3]{0:T(128)S(1)}, s32[3]{0:T(128)}, u32[]{:S(2)}) copy-start(s32[3]{0:T(128)} %pad_add_fusion.refs_0_.role) | copy-start | bytes 40

commit v5 on v4

--- a/solution.py
+++ b/solution.py
@@ -481,8 +481,8 @@
 INS = 6
 DIAGS = 4
 ZERO_ROWS = 256
-HOME_PARTS = (0, 4, 9, 14)
-AWAY_PARTS = (0, 3, 6, 8)
+HOME_PARTS = (0, 0, 4, 9, 14)
+AWAY_PARTS = (0, 3, 5, 7, 8)
 
 
 class Blocks:
@@ -553,7 +553,7 @@
 
 
 def assemble_kernel(sz, number, *refs):
-    first, late_mine, late_theirs = number == 0, None, None
+    late_mine = late_theirs = None
     role, psd, rsd, psm, rsm, co = refs[:6]
     if AWAY_PARTS[number + 1] == sz.layers:
         late_mine, late_theirs = refs[6:8]
@@ -566,6 +566,7 @@
     @pl.when(role[0] == 0)
     def _():
         lo, hi = HOME_PARTS[number:number + 2]
+        first = lo == 0 and hi > 0
         per = sz.rows // ZERO_ROWS
 
         def zero(n):
@@ -814,7 +815,8 @@
         hi_too = lax.ppermute(hi, axes, home_y)
         out = assemble(sz, 0, role, parts)
         out = assemble(sz, 1, role, parts, (), out)
-        out = assemble(sz, 2, role, parts, (late_diag, theirs), out)
+        out = assemble(sz, 2, role, parts, (), out)
+        out = assemble(sz, 3, role, parts, (late_diag, theirs), out)
         out = finish(sz, False, role, (lo, hi, lo_too), parts[-1], out)
         out = finish(sz, True, role, (hi_too,), parts[-1], out)
         return out[None]

time: 1540 us -> 1540 us (level)
    pallas_call x3 -> x4, Pallas kernels: 53.1 us -> 53.9 us  [assemble(): pl.pallas_call(functools.partial(assemble_kernel, sz, number), out_shape=...]
where the time goes in v5:
time: 1540 us; the launch traced here: 1520 us
  Pallas kernels  1500 us (97%)
    pallas_call x1, Pallas kernels, exchange(): pl.pallas_call(functools.partial(exchange_kernel, sz), name='exchange', o...  1440 us
    pallas_call x4, Pallas kernels, assemble(): pl.pallas_call(functools.partial(assemble_kernel, sz, number), out_shape=...  53.9 us
  transfers between devices with their start and end apart: 5, of which 1 were waited for; matrix products, arithmetic and copies ran while one was open for 0% of the time, Pallas kernels for 4%

profile of v5, /device:TPU:1, one launch (start us, length us, event | category | flops | bytes accessed | tf_op | source)
XLA Modules:
  0.0 1522.3 jit_solution(7727280719253612984)
XLA Ops:
  0.0 1440.4 %exchange.1 = (bf16[4,1024,7168]{2,1,0:T(8,128)(2,1)}, bf16[8,1024,7168]{2,1,0:T(8,128)(2,1)}, bf16[4,1024,7168]{2,1,0:T(8,128)(2,1)}, f32[2,8,4112,128]{3,2,1,0...) custom-call(bf16[8,1024,7168]{2,1,0:T(8,128)(2,1)} %a.1), custom_call_target="tpu_custom_call" | custom-call | tf_op jit(solution)/shard_map/exchange/pallas_call | solution.py:459
  1440.4 1.3 collective-permute-start
  1441.7 1.3 collective-permute-start.2
  1443.0 2.0 collective-permute-start.4
  1444.9 0.6 pad_add_fusion.refs_0_.role
  1445.5 0.8 shard_map.17.refs_6_
  1446.4 22.1 %shard_map.18.refs_6_ = f32[3,8,1024,1024]{3,2,1,0:T(8,128)} custom-call(s32[3]{0:T(128)} %pad_add_fusion.refs_0_.role, f32[2,8,4112,128]{3,2,1,0:T(8,128)} %get-tuple-element.16.refs_1_, f32[2,8,4112,128]{3,2,1,0:T(8,128)} %get-tuple-element.17.refs_2_, f32[8,8,1024,128]{3,2,1,0:T(8,128)} %bitcast.7, ...), custom_call_target="tpu_custom_call", output_to_operand_aliasing={{}: (6, {})} | custom-call | flops 10000000000 | bytes 67108864 | tf_op jit(solution)/shard_map/pallas_call | solution.py:690
  1468.5 0.0 collective-permute-done.refs_1_
  1468.5 2.7 collective-permute-start.1
  1471.2 7.8 collective-permute-done.2.refs_0_
  1479.0 2.7 collective-permute-start.3
  1481.7 15.7 %shard_map.19.refs_8_ = f32[3,8,1024,1024]{3,2,1,0:T(8,128)} custom-call(s32[3]{0:T(128)} %pad_add_fusion.refs_0_.role, f32[2,8,4112,128]{3,2,1,0:T(8,128)} %get-tuple-element.16.refs_1_, f32[2,8,4112,128]{3,2,1,0:T(8,128)} %get-tuple-element.17.refs_2_, f32[8,8,1024,128]{3,2,1,0:T(8,128)} %bitcast.8, ...), custom_call_target="tpu_custom_call", output_to_operand_aliasing={{}: (6, {})} | custom-call | flops 10000000000 | bytes 67108864 | tf_op jit(solution)/shard_map/pallas_call | solution.py:690
  1497.3 0.0 copy-start
  1497.3 0.0 collective-permute-done.4.refs_7_
  1497.4 15.3 %shard_map.20.refs_4_ = f32[3,8,1024,1024]{3,2,1,0:T(8,128)} custom-call(s32[3]{0:T(128)} %pad_add_fusion.refs_0_.role, f32[2,8,4112,128]{3,2,1,0:T(8,128)} %get-tuple-element.16.refs_1_, f32[2,8,4112,128]{3,2,1,0:T(8,128)} %get-tuple-element.17.refs_2_, f32[8,8,1024,128]{3,2,1,0:T(8,128)} %bitcast.9, ...), custom_call_target="tpu_custom_call", output_to_operand_aliasing={{}: (8, {})} | custom-call | flops 10000000000 | bytes 67108864 | tf_op jit(solution)/shard_map/pallas_call | solution.py:690
  1512.6 0.0 collective-permute-done.3.refs_2_
  1512.7 0.0 copy-done
  1512.7 6.2 finish.1.refs_2_
  1518.9 0.0 collective-permute-done.1.refs_0_
  1518.9 3.4 finish_last.1
Async XLA Ops:
  1440.4 28.1 %collective-permute-start = (f32[3,1024,128]{2,1,0:T(8,128)}, f32[3,1024,128]{2,1,0:T(8,128)}, u32[]{:S(2)}, u32[]{:S(2)}) collective-permute-start(f32[3,1024,128]{2,1,0:T(8,128)} %get-tuple-element.13), channel_id=1, source_target_pairs={{0,2},{3,1},{4,6},{7,5}} | collective-permute-start | bytes 4718600 | tf_op jit(solution)/shard_map/ppermute | solution.py:812
  1441.7 37.3 %collective-permute-start.2 = (f32[3,1024,128]{2,1,0:T(8,128)}, f32[3,1024,128]{2,1,0:T(8,128)}, u32[]{:S(2)}, u32[]{:S(2)}) collective-permute-start(f32[3,1024,128]{2,1,0:T(8,128)} %get-tuple-element.15), channel_id=1, source_target_pairs={{0,2},{3,1},{4,6},{7,5}} | collective-permute-start | bytes 4718600 | tf_op jit(solution)/shard_map/ppermute | solution.py:811
  1443.0 54.4 %collective-permute-start.4 = (f32[4112,128]{1,0:T(8,128)}, f32[4112,128]{1,0:T(8,128)}, u32[]{:S(2)}, u32[]{:S(2)}) collective-permute-start(f32[4112,128]{1,0:T(8,128)} %get-tuple-element.20.refs_6_), channel_id=1, source_target_pairs={{0,4},{3,7},{4,0},{7,3}} | collective-permute-start | bytes 6316040 | tf_op jit(solution)/shard_map/ppermute | solution.py:813
  1468.5 50.4 %collective-permute-start.1 = (f32[3,1024,128]{2,1,0:T(8,128)}, f32[3,1024,128]{2,1,0:T(8,128)}, u32[]{:S(2)}, u32[]{:S(2)}) collective-permute-start(f32[3,1024,128]{2,1,0:T(8,128)} %collective-permute-done.refs_1_), channel_id=1, source_target_pairs={{1,5},{2,6},{5,1},{6,2}} | collective-permute-start | bytes 4718600 | tf_op jit(solution)/shard_map/ppermute | solution.py:815
  1479.0 33.7 %collective-permute-start.3 = (f32[3,1024,128]{2,1,0:T(8,128)}, f32[3,1024,128]{2,1,0:T(8,128)}, u32[]{:S(2)}, u32[]{:S(2)}) collective-permute-start(f32[3,1024,128]{2,1,0:T(8,128)} %collective-permute-done.2.refs_0_), channel_id=1, source_target_pairs={{1,5},{2,6},{5,1},{6,2}} | collective-permute-start | bytes 4718600 | tf_op jit(solution)/shard_map/ppermute | solution.py:814
  1497.3 15.3 %copy-start = (s32[3]{0:T(128)S(1)}, s32[3]{0:T(128)}, u32[]{:S(2)}) copy-start(s32[3]{0:T(128)} %pad_add_fusion.refs_0_.role) | copy-start | bytes 40
